TPU v7x, 256 devices: a whole 4x4x8 slice. The times are simulated.
256 devices in a mesh: grp: 4 (over y), gx: 16 (over z, core), gy: 4 (over x).
Axes of the slice: x: 4, y: 4, z: 8, core: 2. Of those that a mesh axis runs over, the one named last changes fastest.
Arguments:
- pressure: float32 [4, 64, 64, 128], P('grp', 'gx', 'gy'), may hold values from -6 to 6
- source: float32 [4, 64, 64, 128], P('grp', 'gx', 'gy'), may hold values from -6 to 6
- storage: float32 [4, 64, 64, 128], P('grp', 'gx', 'gy'), may hold values from 0.05 to 2
- well_mask: int32 [4, 64, 64, 128], P('grp', 'gx', 'gy'), may hold values 0 or 1
- block_id: int32 [4, 64, 64, 128], P('grp', 'gx', 'gy'), may hold values from 0 to 63
- basis_weight: float32 [4, 8, 64, 64, 128], P('grp', None, 'gx', 'gy'), may hold values from 0 to 1
- host_elem: int32 [4, 64, 64, 128], P('grp', 'gx', 'gy'), may hold values from 0 to 8191
- displacement: float32 [4, 3, 64, 64, 128], P('grp', None, 'gx', 'gy'), may hold values from -4 to 4
- body_force: float32 [4, 3, 64, 64, 128], P('grp', None, 'gx', 'gy'), may hold values from -6 to 6
- modulus: float32 [4, 64, 64, 128], P('grp', 'gx', 'gy'), may hold values from 0.5 to 4
- elem_mask: int32 [4, 64, 64, 128], P('grp', 'gx', 'gy'), may hold values 0 or 1
- stiffness: float32 [24, 24], replicated, as said below
Outputs:
- pressure_out: float32 [4, 64, 64, 128], P('grp', 'gx', 'gy')
- displacement_out: float32 [4, 3, 64, 64, 128], P('grp', None, 'gx', 'gy')
Inputs may be any that keep to these rules, and one draw needn't show every extreme that they name: stiffness is symmetric and each diagonal entry exceeds the sum of the magnitudes of the other entries in its row by one.
All inputs are finite; a program needn't handle non-finite values. No bound on the sum of `well_mask` or of `elem_mask` on one device may be relied on, other than what follows from the above.
Results may differ from a plain program's by a relative error of at most 0.0003.
Values sent between devices are 32-bit elements; how exact they have to be, the bound alone decides.
A program may use at most 64 MiB of HBM per device.

v0:
```python
import jax
import jax.numpy as jnp
from jax import lax
from jax.sharding import PartitionSpec as P

NBLK = 64
SWEEPS = 2
ITERS = 2


biot_coef = 1.5
relaxation = 0.8
spring_coef = 0.5
well_index = 4.0
highest = lax.Precision.HIGHEST


def passed_along(value, axis, steps):
    count = lax.axis_size(axis)
    leading, last = (max(0, -steps), min(count, count - steps))
    return lax.ppermute(value, axis, [(source, source + steps) for source in range(leading, last)])


def from_everyone(array, axis):
    copies = jnp.broadcast_to(array, (lax.axis_size(axis), *array.shape))
    return lax.all_to_all(copies, axis, split_axis=0, concat_axis=0, tiled=True)


def over_copies(array, axis):
    everything = from_everyone(array, axis)
    return jnp.sum(everything, axis=0)


def packed_total(arrays, axis):
    ravelled, at, gathered = (jnp.concatenate([a.reshape(-1) for a in arrays]), 0, [])
    so_far = over_copies(ravelled, axis)
    for a in arrays:
        gathered.append(so_far[at : at + a.size].reshape(a.shape))
        at += a.size
    return tuple(gathered)


def picked(array, axis, root):
    return lax.dynamic_index_in_dim(lax.all_gather(array, axis), root, 0, keepdims=False)


def padded_2(array, sides, width):
    edges = {}
    for axis, dim in sides:
        devices, length = (lax.axis_size(axis), array.shape[dim])
        up = [(i, (i + 1) % devices) for i in range(devices - 1)]
        last = lax.slice_in_dim(array, length - width, length, axis=dim)
        leading = lax.slice_in_dim(array, 0, width, axis=dim)
        edges[dim] = (
            lax.ppermute(last, axis, up),
            lax.ppermute(leading, axis, [(b, a) for a, b in up]),
        )
    done = []
    for _, dim in sides:
        low, high = edges[dim]
        around = [(width, width) if d in done else (0, 0) for d in range(array.ndim)]
        array = jnp.concatenate([jnp.pad(low, around), array, jnp.pad(high, around)], axis=dim)
        done.append(dim)
    return array


def coupling_vector():
    index = jnp.arange(24, dtype=jnp.int32)
    corner = index // 3
    component = index % 3
    bitval = corner >> 2 - component & 1
    return (bitval.astype(jnp.float32) * 2.0 - 1.0) * 0.25


def corner_list():
    return [(corner >> 2 & 1, corner >> 1 & 1, corner & 1) for corner in range(8)]


def spread(nodes):
    size_x, size_y, size_z = nodes.shape[1:]
    right = passed_along(nodes[:, :1], "gx", -1)
    extended = jnp.concatenate([nodes, right], 1)
    upper = passed_along(extended[:, :, :1], "gy", -1)
    extended = jnp.concatenate([extended, upper], 2)
    extended = jnp.pad(extended, ((0, 0), (0, 0), (0, 0), (0, 1)))
    pieces = [
        extended[
            :, shift_x : shift_x + size_x, shift_y : shift_y + size_y, shift_z : shift_z + size_z
        ]
        for shift_x, shift_y, shift_z in corner_list()
    ]
    return jnp.stack(pieces).reshape(24, size_x * size_y * size_z)


def assemble(values, shape):
    size_x, size_y, size_z = shape
    parts = values.reshape(8, 3, size_x, size_y, size_z)
    total = jnp.zeros((3, size_x + 1, size_y + 1, size_z + 1), jnp.float32)
    for corner, (shift_x, shift_y, shift_z) in enumerate(corner_list()):
        total = total + jnp.pad(
            parts[corner],
            ((0, 0), (shift_x, 1 - shift_x), (shift_y, 1 - shift_y), (shift_z, 1 - shift_z)),
        )
    total = total[:, :, :, :size_z]
    moved = passed_along(total[:, size_x:], "gx", 1)
    inner = total[:, :size_x]
    inner = jnp.concatenate([inner[:, :1] + moved, inner[:, 1:]], 1)
    moved = passed_along(inner[:, :, size_y:], "gy", 1)
    inner = inner[:, :, :size_y]
    return jnp.concatenate([inner[:, :, :1] + moved, inner[:, :, 1:]], 2)


def two_sums(remain, image):
    return packed_total((jnp.sum(remain * remain), jnp.sum(remain * image)), ("gx", "gy"))


def local(
    pressure,
    source,
    storage,
    well_mask,
    block_id,
    basis_weight,
    host_elem,
    displacement,
    body_force,
    modulus,
    elem_mask,
    stiffness,
):
    groups = lax.axis_size("grp")
    group_index = lax.axis_index("grp")
    is_mech = group_index == groups - 1
    is_top = group_index == groups - 2
    flow_keep = jnp.where(is_mech, 0.0, 1.0).astype(jnp.float32)
    top_keep = jnp.where(is_top, 0.0, 1.0).astype(jnp.float32)
    start = pressure[0]
    shape = start.shape
    elements = shape[0] * shape[1] * shape[2]
    coupling = coupling_vector()
    mech_mask = elem_mask[0].astype(jnp.float32).reshape(-1)
    weights = modulus[0].reshape(-1) * mech_mask

    def apply(vector):
        return (
            assemble(
                jnp.dot(stiffness, spread(vector), precision=highest) * weights[None, :], shape
            )
            + spring_coef * vector
        )

    initial = displacement[0]
    strain = mech_mask * jnp.dot(coupling, spread(initial), precision=highest)
    strain = picked(strain, "grp", groups - 1)
    hosts = host_elem[0].reshape(-1)
    strain_cells = jnp.take(strain, hosts).reshape(shape)
    diagonal = 6.0 + storage[0] + well_index * well_mask[0].astype(jnp.float32)
    forcing = source[0] - biot_coef * strain_cells

    def neighbours(field):
        padded = padded_2(field, (("grp", 2), ("gx", 0), ("gy", 1)), 1)
        padded = jnp.concatenate([padded[:, :, :-1], padded[:, :, -1:] * top_keep], 2)
        total = padded[2:, 1:-1, 1:-1] + padded[:-2, 1:-1, 1:-1]
        total = total + padded[1:-1, 2:, 1:-1] + padded[1:-1, :-2, 1:-1]
        return total + padded[1:-1, 1:-1, 2:] + padded[1:-1, 1:-1, :-2]

    def residual(field):
        return forcing - (diagonal * field - neighbours(field))

    current = start
    for sweep_index in range(SWEEPS):
        current = current + relaxation * residual(current) / diagonal
    remainder = residual(current).reshape(-1)
    onehot = (block_id[0].reshape(1, -1) == jnp.arange(NBLK, dtype=jnp.int32)[:, None]).astype(
        jnp.float32
    )
    weight_flat = basis_weight[0].reshape(8, -1)
    coarse = jnp.einsum("bc,jc->bj", onehot, weight_flat * remainder, precision=highest)
    scale = 1.0 + jnp.einsum(
        "bc,jc->bj", onehot, weight_flat * weight_flat * diagonal.reshape(1, -1), precision=highest
    )
    correction = coarse / scale
    spread_back = jnp.dot(correction.T, onehot, precision=highest)
    updated = current + jnp.sum(weight_flat * spread_back, axis=0).reshape(shape)
    change = ((updated - start) * flow_keep).reshape(-1)
    sums = jax.ops.segment_sum(change, hosts, num_segments=elements)
    counts = jax.ops.segment_sum(
        jnp.broadcast_to(flow_keep, change.shape), hosts, num_segments=elements
    )
    sums, counts = packed_total((sums, counts), "grp")
    element_pressure = sums / jnp.maximum(counts, 1.0)
    force = body_force[0] + biot_coef * assemble(
        coupling[:, None] * (mech_mask * element_pressure)[None, :], shape
    )
    solution = initial
    remain = force - apply(solution)
    image = apply(remain)
    norm_now, product = two_sums(remain, image)
    step_size = norm_now / product
    search, along = (remain, image)
    for iteration in range(ITERS):
        solution = solution + step_size * search
        remain = remain - step_size * along
        if iteration + 1 < ITERS:
            image = apply(remain)
            norm_next, product = two_sums(remain, image)
            ratio = norm_next / norm_now
            step_size = norm_next / (product - ratio * norm_next / step_size)
            search = remain + ratio * search
            along = image + ratio * along
            norm_now = norm_next
    pressure_out = jnp.where(is_mech, 0.0, updated)[None]
    displacement_out = jnp.where(is_mech, solution, 0.0)[None]
    return (pressure_out, displacement_out)


def solution(mesh):
    placed = (
        P("grp", "gx", "gy", None),
        P("grp", "gx", "gy", None),
        P("grp", "gx", "gy", None),
        P("grp", "gx", "gy", None),
        P("grp", "gx", "gy", None),
        P("grp", None, "gx", "gy", None),
        P("grp", "gx", "gy", None),
        P("grp", None, "gx", "gy", None),
        P("grp", None, "gx", "gy", None),
        P("grp", "gx", "gy", None),
        P("grp", "gx", "gy", None),
        P(),
    )
    return jax.shard_map(
        local,
        mesh=mesh,
        in_specs=placed,
        out_specs=(P("grp", "gx", "gy", None), P("grp", None, "gx", "gy", None)),
        check_vma=False,
    )
```

profile of v0, /device:TPU:24, one launch (start us, length us, event | category | flops | bytes accessed | tf_op | source)
XLA Modules:
  0.0 343.5 jit_solution(17057426245447658689)
XLA Ops:
  1.6 1.3 collective-permute-start.2
  7.0 3.0 collective-permute-start.5
  10.0 4.5 %collective-permute-start.7 = (f32[4,1,128]{2,1,0:T(1,128)S(1)}, f32[4,1,128]{2,1,0:T(1,128)S(1)}, u32[]{:S(2)}, u32[]{:S(2)}) collective-permute-start(f32[4,1,128]{2,1,0:T(1,128)S(1)} %get-tuple-element.61), channel_id=1, source_target_pairs={{0,1},{1,2},{2,3},{4,5},{5,6},{6,7},{8,9},{9,10},{10,11},{12,13},{... | collective-permute-start | bytes 6152 | tf_op jit(solution)/shard_map/ppermute | solution.py:55
  17.9 43.2 %scatter_custom_fusion.1 = f32[8192]{0:T(1024)S(1)} fusion(s32[8192]{0:T(1024)S(1)} %bitcast.357, f32[8192]{0:T(1024)S(1)} %broadcast.266, f32[]{:T(128)} %constant.31.clone.1), kind=kCustom, calls=%fused_computation.255 | custom fusion | flops 8192 | bytes 32772 | tf_op jit(solution)/shard_map/scatter-add | solution.py:187
  61.1 4.5 %collective-permute-start.3 = (f32[4,16,1]{2,1,0:T(8,128)S(1)}, f32[4,16,1]{2,1,0:T(8,128)S(1)}, u32[]{:S(2)}, u32[]{:S(2)}) collective-permute-start(f32[4,16,1]{2,1,0:T(8,128)S(1)} %get-tuple-element.65), channel_id=1, source_target_pairs={{64,0},{128,64},{192,128},{65,1},{129,65},{193,129},{66,2},{130,66... | collective-permute-start | bytes 776 | tf_op jit(solution)/shard_map/ppermute | solution.py:56
  65.7 1.3 collective-permute-start
  67.4 1.9 collective-permute-done
  69.3 1.3 collective-permute-start.1
  70.7 4.1 %collective-permute-done.1 = f32[3,5,1,128]{3,2,1,0:T(1,128)S(1)} collective-permute-done((f32[3,5,1,128]{3,2,1,0:T(1,128)S(1)}, f32[3,5,1,128]{3,2,1,0:T(1,128)S(1)}, u32[]{:S(2)}, u32[]{:S(2)}) %collective-permute-start.1) | collective-permute-done | bytes 7712 | tf_op jit(solution)/shard_map/ppermute | solution.py:21
  76.0 12.0 %all-gather = f32[32768]{0:T(1024)S(1)} all-gather(f32[8192]{0:T(1024)S(1)} %mul.235), channel_id=2, replica_groups=mesh['grp'=4,'gx'=16,'gy'=4] {'grp'}, dimensions={0}, use_global_device_ids=true | all-gather | bytes 163840 | tf_op jit(solution)/shard_map/all_gather | solution.py:44
  88.0 45.5 %gather_fusion = f32[8192]{0:T(1024)S(1)} fusion(f32[8192]{0:T(1024)S(1)} %slice.680, s32[8192]{0:T(1024)S(1)} %broadcast_clamp_fusion), kind=kCustom, calls=%fused_computation | custom fusion | bytes 98304 | tf_op jit(solution)/shard_map/jit(_take)/gather | solution.py:156
  133.8 1.3 collective-permute-start.8
  135.1 1.3 collective-permute-start.12
  136.4 1.3 collective-permute-start.10
  137.7 3.0 collective-permute-start.11
  140.8 4.5 %collective-permute-start.13 = (f32[4,1,128]{2,1,0:T(1,128)S(1)}, f32[4,1,128]{2,1,0:T(1,128)S(1)}, u32[]{:S(2)}, u32[]{:S(2)}) collective-permute-start(f32[4,1,128]{2,1,0:T(1,128)S(1)} %get-tuple-element.55), channel_id=1, source_target_pairs={{0,1},{1,2},{2,3},{4,5},{5,6},{6,7},{8,9},{9,10},{10,11},{12,13},{... | collective-permute-start | bytes 6152 | tf_op jit(solution)/shard_map/ppermute | solution.py:55
  146.5 4.5 %collective-permute-start.9 = (f32[4,16,1]{2,1,0:T(8,128)S(1)}, f32[4,16,1]{2,1,0:T(8,128)S(1)}, u32[]{:S(2)}, u32[]{:S(2)}) collective-permute-start(f32[4,16,1]{2,1,0:T(8,128)S(1)} %get-tuple-element.59), channel_id=1, source_target_pairs={{64,0},{128,64},{192,128},{65,1},{129,65},{193,129},{66,2},{130,66... | collective-permute-start | bytes 776 | tf_op jit(solution)/shard_map/ppermute | solution.py:56
  153.0 1.3 collective-permute-start.18
  154.3 1.3 collective-permute-start.16
  155.6 3.6 %collective-permute-start.17 = (f32[1,16,128]{2,1,0:T(8,128)S(1)}, f32[1,16,128]{2,1,0:T(8,128)S(1)}, u32[]{:S(2)}, u32[]{:S(2)}) collective-permute-start(f32[1,16,128]{2,1,0:T(8,128)S(1)} %get-tuple-element.51), channel_id=1, source_target_pairs={{0,4},{4,8},{8,12},{12,16},{16,20},{20,24},{24,28},{28,32},{32,36}... | collective-permute-start | bytes 24584 | tf_op jit(solution)/shard_map/ppermute | solution.py:55
  159.1 4.3 %collective-permute-start.19 = (f32[4,1,128]{2,1,0:T(1,128)S(1)}, f32[4,1,128]{2,1,0:T(1,128)S(1)}, u32[]{:S(2)}, u32[]{:S(2)}) collective-permute-start(f32[4,1,128]{2,1,0:T(1,128)S(1)} %get-tuple-element.49), channel_id=1, source_target_pairs={{0,1},{1,2},{2,3},{4,5},{5,6},{6,7},{8,9},{9,10},{10,11},{12,13},{... | collective-permute-start | bytes 6152 | tf_op jit(solution)/shard_map/ppermute | solution.py:55
  163.5 1.3 collective-permute-start.14
  164.8 4.6 %collective-permute-start.15 = (f32[4,16,1]{2,1,0:T(8,128)S(1)}, f32[4,16,1]{2,1,0:T(8,128)S(1)}, u32[]{:S(2)}, u32[]{:S(2)}) collective-permute-start(f32[4,16,1]{2,1,0:T(8,128)S(1)} %get-tuple-element.53), channel_id=1, source_target_pairs={{64,0},{128,64},{192,128},{65,1},{129,65},{193,129},{66,2},{130,66... | collective-permute-start | bytes 776 | tf_op jit(solution)/shard_map/ppermute | solution.py:56
  173.8 43.2 %scatter_custom_fusion = f32[8192]{0:T(1024)S(1)} fusion(s32[8192]{0:T(1024)S(1)} %bitcast.358, f32[8192]{0:T(1024)S(1)} %bitcast.366, f32[]{:T(128)} %constant.31.clone.1), kind=kCustom, calls=%fused_computation.257 | custom fusion | flops 8192 | bytes 32772 | tf_op jit(solution)/shard_map/scatter-add | solution.py:186
  217.9 6.5 %all-to-all-start = ((f32[4,1,16384]{2,1,0:T(1,128)}), f32[4,1,16384]{2,1,0:T(1,128)S(1)}, u32[]{:S(2)}, u32[]{:S(2)}) async-start(f32[4,1,16384]{2,1,0:T(1,128)} %broadcast_in_dim.40), calls=%async_computation | async-start | bytes 524288 | tf_op jit(solution)/shard_map/all_to_all | solution.py:26
  224.4 5.6 %all-to-all-done = f32[4,1,16384]{2,1,0:T(1,128)S(1)} async-done(((f32[4,1,16384]{2,1,0:T(1,128)}), f32[4,1,16384]{2,1,0:T(1,128)S(1)}, u32[]{:S(2)}, u32[]{:S(2)}) %all-to-all-start) | async-done | bytes 262176 | tf_op jit(solution)/shard_map/all_to_all | solution.py:26
  232.3 1.8 collective-permute-start.22
  235.0 4.9 %collective-permute-start.20 = (f32[3,1,17,128]{3,2,1,0:T(8,128)S(1)}, f32[3,1,17,128]{3,2,1,0:T(8,128)S(1)}, u32[]{:S(2)}, u32[]{:S(2)}) collective-permute-start(f32[3,1,17,128]{3,2,1,0:T(8,128)S(1)} %slice.714), channel_id=1, source_target_pairs={{0,4},{4,8},{8,12},{12,16},{16,20},{20,24},{24,28},{28,32},{32,36}... | collective-permute-start | bytes 78344 | tf_op jit(solution)/shard_map/ppermute | solution.py:21
  240.0 3.4 collective-permute-start.23
  243.5 3.4 collective-permute-start.21
  246.9 1.3 collective-permute-done.21
  248.3 1.3 collective-permute-start.24
  249.6 1.8 collective-permute-done.24
  251.4 1.3 collective-permute-start.25
  252.7 4.5 %collective-permute-done.25 = f32[3,5,1,128]{3,2,1,0:T(1,128)S(1)} collective-permute-done((f32[3,5,1,128]{3,2,1,0:T(1,128)S(1)}, f32[3,5,1,128]{3,2,1,0:T(1,128)S(1)}, u32[]{:S(2)}, u32[]{:S(2)}) %collective-permute-start.25) | collective-permute-done | bytes 7712 | tf_op jit(solution)/shard_map/ppermute | solution.py:21
  259.3 3.5 %collective-permute-start.26 = (f32[3,1,17,128]{3,2,1,0:T(8,128)S(1)}, f32[3,1,17,128]{3,2,1,0:T(8,128)S(1)}, u32[]{:S(2)}, u32[]{:S(2)}) collective-permute-start(f32[3,1,17,128]{3,2,1,0:T(8,128)S(1)} %slice.739), channel_id=1, source_target_pairs={{0,4},{4,8},{8,12},{12,16},{16,20},{20,24},{24,28},{28,32},{32,36}... | collective-permute-start | bytes 78344 | tf_op jit(solution)/shard_map/ppermute | solution.py:21
  263.6 3.6 %collective-permute-start.27 = (f32[3,4,1,128]{3,2,1,0:T(1,128)S(1)}, f32[3,4,1,128]{3,2,1,0:T(1,128)S(1)}, u32[]{:S(2)}, u32[]{:S(2)}) collective-permute-start(f32[3,4,1,128]{3,2,1,0:T(1,128)S(1)} %pad_maximum_fusion.71), channel_id=1, source_target_pairs={{0,1},{1,2},{2,3},{4,5},{5,6},{6,7},{8,9},{9,10},{10,11},{12,13},{... | collective-permute-start | bytes 18440 | tf_op jit(solution)/shard_map/ppermute | solution.py:21
  267.3 1.3 collective-permute-done.27
  269.3 1.4 pad_maximum_fusion.74
  270.7 24.5 %all_to_all.18 = f32[64,1,2]{2,1,0:T(1,128)S(1)} all-to-all(f32[64,1,2]{2,1,0:T(1,128)S(1)} %broadcast_in_dim.41), channel_id=1, replica_groups=mesh['grp'=4,'gx'=16,'gy'=4] {'gx','gy'}, dimensions={0} | all-to-all | bytes 1024 | tf_op jit(solution)/shard_map/all_to_all | solution.py:26
  297.3 1.3 collective-permute-start.28
  298.6 1.8 collective-permute-done.28
  301.7 4.2 %collective-permute-done.29 = f32[3,5,1,128]{3,2,1,0:T(1,128)S(1)} collective-permute-done((f32[3,5,1,128]{3,2,1,0:T(1,128)S(1)}, f32[3,5,1,128]{3,2,1,0:T(1,128)S(1)}, u32[]{:S(2)}, u32[]{:S(2)}) %collective-permute-start.29) | collective-permute-done | bytes 7712 | tf_op jit(solution)/shard_map/ppermute | solution.py:21
  308.0 2.4 collective-permute-start.30
  311.3 2.5 collective-permute-start.31
  313.8 1.3 collective-permute-done.31
  315.8 1.3 pad_maximum_fusion.75
  317.1 20.4 %all_to_all.19 = f32[64,1,2]{2,1,0:T(1,128)S(1)} all-to-all(f32[64,1,2]{2,1,0:T(1,128)S(1)} %broadcast_in_dim.42), channel_id=1, replica_groups=mesh['grp'=4,'gx'=16,'gy'=4] {'gx','gy'}, dimensions={0} | all-to-all | bytes 1024 | tf_op jit(solution)/shard_map/all_to_all | solution.py:26
  (220 shorter events, 32.0 us)
Async XLA Ops:
  0.6 229.7 %copy-start = (f32[24,24]{1,0:T(8,128)S(1)}, f32[24,24]{1,0:T(8,128)}, u32[]{:S(2)}) copy-start(f32[24,24]{1,0:T(8,128)} %param.23) | copy-start | bytes 6916
  0.6 66.6 %copy-start.2 = (f32[1,4,16,128]{3,2,1,0:T(8,128)S(1)}, f32[1,4,16,128]{3,2,1,0:T(8,128)}, u32[]{:S(2)}) copy-start(f32[1,4,16,128]{3,2,1,0:T(8,128)} %param.12) | copy-start | bytes 98308
  0.7 17.2 %copy-start.5 = (s32[1,4,16,128]{3,2,1,0:T(8,128)S(1)}, s32[1,4,16,128]{3,2,1,0:T(8,128)}, u32[]{:S(2)}) copy-start(s32[1,4,16,128]{3,2,1,0:T(8,128)} %param.18) | copy-start | bytes 98308
  0.7 17.1 %copy-start.4 = (f32[1,8,4,16,128]{4,3,2,1,0:T(8,128)S(1)}, f32[1,8,4,16,128]{4,3,2,1,0:T(8,128)}, u32[]{:S(2)}) copy-start(f32[1,8,4,16,128]{4,3,2,1,0:T(8,128)} %param.17) | copy-start | bytes 786436
  0.7 68.6 %copy-start.1 = (f32[1,3,4,16,128]{4,3,2,1,0:T(8,128)S(1)}, f32[1,3,4,16,128]{4,3,2,1,0:T(8,128)}, u32[]{:S(2)}) copy-start(f32[1,3,4,16,128]{4,3,2,1,0:T(8,128)} %param.19) | copy-start | bytes 294916
  1.6 65.6 %collective-permute-start.2 = (f32[4,16,1]{2,1,0:T(8,128)S(1)}, f32[4,16,1]{2,1,0:T(8,128)S(1)}, u32[]{:S(2)}, u32[]{:S(2)}) collective-permute-start(f32[4,16,1]{2,1,0:T(8,128)S(1)} %get-tuple-element.66), channel_id=1, source_target_pairs={{0,64},{64,128},{128,192},{1,65},{65,129},{129,193},{2,66},{66,130... | collective-permute-start | bytes 776 | tf_op jit(solution)/shard_map/ppermute | solution.py:55
  3.7 57.4 %collective-permute-start.6 = (f32[4,1,128]{2,1,0:T(1,128)S(1)}, f32[4,1,128]{2,1,0:T(1,128)S(1)}, u32[]{:S(2)}, u32[]{:S(2)}) collective-permute-start(f32[4,1,128]{2,1,0:T(1,128)S(1)} %get-tuple-element.62), channel_id=1, source_target_pairs={{1,0},{2,1},{3,2},{5,4},{6,5},{7,6},{9,8},{10,9},{11,10},{13,12},{... | collective-permute-start | bytes 6152 | tf_op jit(solution)/shard_map/ppermute | solution.py:56
  5.7 61.4 %collective-permute-start.4 = (f32[1,16,128]{2,1,0:T(8,128)S(1)}, f32[1,16,128]{2,1,0:T(8,128)S(1)}, u32[]{:S(2)}, u32[]{:S(2)}) collective-permute-start(f32[1,16,128]{2,1,0:T(8,128)S(1)} %get-tuple-element.64), channel_id=1, source_target_pairs={{4,0},{8,4},{12,8},{16,12},{20,16},{24,20},{28,24},{32,28},{36,32}... | collective-permute-start | bytes 24584 | tf_op jit(solution)/shard_map/ppermute | solution.py:56
  7.0 60.2 %collective-permute-start.5 = (f32[1,16,128]{2,1,0:T(8,128)S(1)}, f32[1,16,128]{2,1,0:T(8,128)S(1)}, u32[]{:S(2)}, u32[]{:S(2)}) collective-permute-start(f32[1,16,128]{2,1,0:T(8,128)S(1)} %get-tuple-element.63), channel_id=1, source_target_pairs={{0,4},{4,8},{8,12},{12,16},{16,20},{20,24},{24,28},{28,32},{32,36}... | collective-permute-start | bytes 24584 | tf_op jit(solution)/shard_map/ppermute | solution.py:55
  10.0 55.7 %collective-permute-start.7 = (f32[4,1,128]{2,1,0:T(1,128)S(1)}, f32[4,1,128]{2,1,0:T(1,128)S(1)}, u32[]{:S(2)}, u32[]{:S(2)}) collective-permute-start(f32[4,1,128]{2,1,0:T(1,128)S(1)} %get-tuple-element.61), channel_id=1, source_target_pairs={{0,1},{1,2},{2,3},{4,5},{5,6},{6,7},{8,9},{9,10},{10,11},{12,13},{... | collective-permute-start | bytes 6152 | tf_op jit(solution)/shard_map/ppermute | solution.py:55
  61.1 6.2 %collective-permute-start.3 = (f32[4,16,1]{2,1,0:T(8,128)S(1)}, f32[4,16,1]{2,1,0:T(8,128)S(1)}, u32[]{:S(2)}, u32[]{:S(2)}) collective-permute-start(f32[4,16,1]{2,1,0:T(8,128)S(1)} %get-tuple-element.65), channel_id=1, source_target_pairs={{64,0},{128,64},{192,128},{65,1},{129,65},{193,129},{66,2},{130,66... | collective-permute-start | bytes 776 | tf_op jit(solution)/shard_map/ppermute | solution.py:56
  65.7 3.6 %collective-permute-start = (f32[3,1,16,128]{3,2,1,0:T(8,128)S(1)}, f32[3,1,16,128]{3,2,1,0:T(8,128)S(1)}, u32[]{:S(2)}, u32[]{:S(2)}) collective-permute-start(f32[3,1,16,128]{3,2,1,0:T(8,128)S(1)} %slice.677), channel_id=1, source_target_pairs={{4,0},{8,4},{12,8},{16,12},{20,16},{24,20},{28,24},{32,28},{36,32}... | collective-permute-start | bytes 73736 | tf_op jit(solution)/shard_map/ppermute | solution.py:21
  69.3 5.5 %collective-permute-start.1 = (f32[3,5,1,128]{3,2,1,0:T(1,128)S(1)}, f32[3,5,1,128]{3,2,1,0:T(1,128)S(1)}, u32[]{:S(2)}, u32[]{:S(2)}) collective-permute-start(f32[3,5,1,128]{3,2,1,0:T(1,128)S(1)} %pad_maximum_fusion.69), channel_id=1, source_target_pairs={{1,0},{2,1},{3,2},{5,4},{6,5},{7,6},{9,8},{10,9},{11,10},{13,12},{... | collective-permute-start | bytes 23048 | tf_op jit(solution)/shard_map/ppermute | solution.py:21
  88.0 45.6 %copy-start.6 = (s32[1,4,16,128]{3,2,1,0:T(8,128)S(1)}, s32[1,4,16,128]{3,2,1,0:T(8,128)}, u32[]{:S(2)}) copy-start(s32[1,4,16,128]{3,2,1,0:T(8,128)} %param.15) | copy-start | bytes 98308
  88.0 45.6 %copy-start.7 = (f32[1,4,16,128]{3,2,1,0:T(8,128)S(1)}, f32[1,4,16,128]{3,2,1,0:T(8,128)}, u32[]{:S(2)}) copy-start(f32[1,4,16,128]{3,2,1,0:T(8,128)} %param.14) | copy-start | bytes 98308
  88.0 45.6 %copy-start.8 = (f32[1,4,16,128]{3,2,1,0:T(8,128)S(1)}, f32[1,4,16,128]{3,2,1,0:T(8,128)}, u32[]{:S(2)}) copy-start(f32[1,4,16,128]{3,2,1,0:T(8,128)} %param.13) | copy-start | bytes 98308
  133.6 11.8 %copy-start.10 = (s32[1,4,16,128]{3,2,1,0:T(8,128)S(1)}, s32[1,4,16,128]{3,2,1,0:T(8,128)}, u32[]{:S(2)}) copy-start(s32[1,4,16,128]{3,2,1,0:T(8,128)} %param.16) | copy-start | bytes 98308
  133.8 17.5 %collective-permute-start.8 = (f32[4,16,1]{2,1,0:T(8,128)S(1)}, f32[4,16,1]{2,1,0:T(8,128)S(1)}, u32[]{:S(2)}, u32[]{:S(2)}) collective-permute-start(f32[4,16,1]{2,1,0:T(8,128)S(1)} %get-tuple-element.60), channel_id=1, source_target_pairs={{0,64},{64,128},{128,192},{1,65},{65,129},{129,193},{2,66},{66,130... | collective-permute-start | bytes 776 | tf_op jit(solution)/shard_map/ppermute | solution.py:55
  135.1 11.3 %collective-permute-start.12 = (f32[4,1,128]{2,1,0:T(1,128)S(1)}, f32[4,1,128]{2,1,0:T(1,128)S(1)}, u32[]{:S(2)}, u32[]{:S(2)}) collective-permute-start(f32[4,1,128]{2,1,0:T(1,128)S(1)} %get-tuple-element.56), channel_id=1, source_target_pairs={{1,0},{2,1},{3,2},{5,4},{6,5},{7,6},{9,8},{10,9},{11,10},{13,12},{... | collective-permute-start | bytes 6152 | tf_op jit(solution)/shard_map/ppermute | solution.py:56
  136.4 14.7 %collective-permute-start.10 = (f32[1,16,128]{2,1,0:T(8,128)S(1)}, f32[1,16,128]{2,1,0:T(8,128)S(1)}, u32[]{:S(2)}, u32[]{:S(2)}) collective-permute-start(f32[1,16,128]{2,1,0:T(8,128)S(1)} %get-tuple-element.58), channel_id=1, source_target_pairs={{4,0},{8,4},{12,8},{16,12},{20,16},{24,20},{28,24},{32,28},{36,32}... | collective-permute-start | bytes 24584 | tf_op jit(solution)/shard_map/ppermute | solution.py:56
  137.7 13.5 %collective-permute-start.11 = (f32[1,16,128]{2,1,0:T(8,128)S(1)}, f32[1,16,128]{2,1,0:T(8,128)S(1)}, u32[]{:S(2)}, u32[]{:S(2)}) collective-permute-start(f32[1,16,128]{2,1,0:T(8,128)S(1)} %get-tuple-element.57), channel_id=1, source_target_pairs={{0,4},{4,8},{8,12},{12,16},{16,20},{20,24},{24,28},{28,32},{32,36}... | collective-permute-start | bytes 24584 | tf_op jit(solution)/shard_map/ppermute | solution.py:55
  140.8 10.3 %collective-permute-start.13 = (f32[4,1,128]{2,1,0:T(1,128)S(1)}, f32[4,1,128]{2,1,0:T(1,128)S(1)}, u32[]{:S(2)}, u32[]{:S(2)}) collective-permute-start(f32[4,1,128]{2,1,0:T(1,128)S(1)} %get-tuple-element.55), channel_id=1, source_target_pairs={{0,1},{1,2},{2,3},{4,5},{5,6},{6,7},{8,9},{9,10},{10,11},{12,13},{... | collective-permute-start | bytes 6152 | tf_op jit(solution)/shard_map/ppermute | solution.py:55
  146.5 6.1 %collective-permute-start.9 = (f32[4,16,1]{2,1,0:T(8,128)S(1)}, f32[4,16,1]{2,1,0:T(8,128)S(1)}, u32[]{:S(2)}, u32[]{:S(2)}) collective-permute-start(f32[4,16,1]{2,1,0:T(8,128)S(1)} %get-tuple-element.59), channel_id=1, source_target_pairs={{64,0},{128,64},{192,128},{65,1},{129,65},{193,129},{66,2},{130,66... | collective-permute-start | bytes 776 | tf_op jit(solution)/shard_map/ppermute | solution.py:56
  153.0 11.8 %collective-permute-start.18 = (f32[4,1,128]{2,1,0:T(1,128)S(1)}, f32[4,1,128]{2,1,0:T(1,128)S(1)}, u32[]{:S(2)}, u32[]{:S(2)}) collective-permute-start(f32[4,1,128]{2,1,0:T(1,128)S(1)} %get-tuple-element.50), channel_id=1, source_target_pairs={{1,0},{2,1},{3,2},{5,4},{6,5},{7,6},{9,8},{10,9},{11,10},{13,12},{... | collective-permute-start | bytes 6152 | tf_op jit(solution)/shard_map/ppermute | solution.py:56
  154.3 15.3 %collective-permute-start.16 = (f32[1,16,128]{2,1,0:T(8,128)S(1)}, f32[1,16,128]{2,1,0:T(8,128)S(1)}, u32[]{:S(2)}, u32[]{:S(2)}) collective-permute-start(f32[1,16,128]{2,1,0:T(8,128)S(1)} %get-tuple-element.52), channel_id=1, source_target_pairs={{4,0},{8,4},{12,8},{16,12},{20,16},{24,20},{28,24},{32,28},{36,32}... | collective-permute-start | bytes 24584 | tf_op jit(solution)/shard_map/ppermute | solution.py:56
  155.6 14.1 %collective-permute-start.17 = (f32[1,16,128]{2,1,0:T(8,128)S(1)}, f32[1,16,128]{2,1,0:T(8,128)S(1)}, u32[]{:S(2)}, u32[]{:S(2)}) collective-permute-start(f32[1,16,128]{2,1,0:T(8,128)S(1)} %get-tuple-element.51), channel_id=1, source_target_pairs={{0,4},{4,8},{8,12},{12,16},{16,20},{20,24},{24,28},{28,32},{32,36}... | collective-permute-start | bytes 24584 | tf_op jit(solution)/shard_map/ppermute | solution.py:55
  159.1 10.3 %collective-permute-start.19 = (f32[4,1,128]{2,1,0:T(1,128)S(1)}, f32[4,1,128]{2,1,0:T(1,128)S(1)}, u32[]{:S(2)}, u32[]{:S(2)}) collective-permute-start(f32[4,1,128]{2,1,0:T(1,128)S(1)} %get-tuple-element.49), channel_id=1, source_target_pairs={{0,1},{1,2},{2,3},{4,5},{5,6},{6,7},{8,9},{9,10},{10,11},{12,13},{... | collective-permute-start | bytes 6152 | tf_op jit(solution)/shard_map/ppermute | solution.py:55
  163.5 6.2 %collective-permute-start.14 = (f32[4,16,1]{2,1,0:T(8,128)S(1)}, f32[4,16,1]{2,1,0:T(8,128)S(1)}, u32[]{:S(2)}, u32[]{:S(2)}) collective-permute-start(f32[4,16,1]{2,1,0:T(8,128)S(1)} %get-tuple-element.54), channel_id=1, source_target_pairs={{0,64},{64,128},{128,192},{1,65},{65,129},{129,193},{2,66},{66,130... | collective-permute-start | bytes 776 | tf_op jit(solution)/shard_map/ppermute | solution.py:55
  164.8 6.2 %collective-permute-start.15 = (f32[4,16,1]{2,1,0:T(8,128)S(1)}, f32[4,16,1]{2,1,0:T(8,128)S(1)}, u32[]{:S(2)}, u32[]{:S(2)}) collective-permute-start(f32[4,16,1]{2,1,0:T(8,128)S(1)} %get-tuple-element.53), channel_id=1, source_target_pairs={{64,0},{128,64},{192,128},{65,1},{129,65},{193,129},{66,2},{130,66... | collective-permute-start | bytes 776 | tf_op jit(solution)/shard_map/ppermute | solution.py:56
  173.2 57.1 %copy-start.9 = (f32[1,4,16,128]{3,2,1,0:T(8,128)S(1)}, f32[1,4,16,128]{3,2,1,0:T(8,128)}, u32[]{:S(2)}) copy-start(f32[1,4,16,128]{3,2,1,0:T(8,128)} %param.21) | copy-start | bytes 98308
  217.9 12.1 %all-to-all-start = ((f32[4,1,16384]{2,1,0:T(1,128)}), f32[4,1,16384]{2,1,0:T(1,128)S(1)}, u32[]{:S(2)}, u32[]{:S(2)}) async-start(f32[4,1,16384]{2,1,0:T(1,128)} %broadcast_in_dim.40), calls=%async_computation | async-start | bytes 524288 | tf_op jit(solution)/shard_map/all_to_all | solution.py:26
  232.3 7.5 %collective-permute-start.22 = (f32[3,1,17,128]{3,1,0,2:T(1,128)S(1)}, f32[3,1,17,128]{3,1,0,2:T(1,128)S(1)}, u32[]{:S(2)}, u32[]{:S(2)}) collective-permute-start(f32[3,1,17,128]{3,1,0,2:T(1,128)S(1)} %slice.725), channel_id=1, source_target_pairs={{0,4},{4,8},{8,12},{12,16},{16,20},{20,24},{24,28},{28,32},{32,36}... | collective-permute-start | bytes 78344 | tf_op jit(solution)/shard_map/ppermute | solution.py:21
  235.0 13.3 %copy-start.3 = (f32[1,3,4,16,128]{4,3,2,1,0:T(8,128)S(1)}, f32[1,3,4,16,128]{4,3,2,1,0:T(8,128)}, u32[]{:S(2)}) copy-start(f32[1,3,4,16,128]{4,3,2,1,0:T(8,128)} %param.20) | copy-start | bytes 294916
  235.0 8.4 %collective-permute-start.20 = (f32[3,1,17,128]{3,2,1,0:T(8,128)S(1)}, f32[3,1,17,128]{3,2,1,0:T(8,128)S(1)}, u32[]{:S(2)}, u32[]{:S(2)}) collective-permute-start(f32[3,1,17,128]{3,2,1,0:T(8,128)S(1)} %slice.714), channel_id=1, source_target_pairs={{0,4},{4,8},{8,12},{12,16},{16,20},{20,24},{24,28},{28,32},{32,36}... | collective-permute-start | bytes 78344 | tf_op jit(solution)/shard_map/ppermute | solution.py:21
  240.0 6.9 %collective-permute-start.23 = (f32[3,4,1,128]{3,1,0,2:T(4,128)S(1)}, f32[3,4,1,128]{3,1,0,2:T(4,128)S(1)}, u32[]{:S(2)}, u32[]{:S(2)}) collective-permute-start(f32[3,4,1,128]{3,1,0,2:T(4,128)S(1)} %pad_maximum_fusion.72), channel_id=1, source_target_pairs={{0,1},{1,2},{2,3},{4,5},{5,6},{6,7},{8,9},{9,10},{10,11},{12,13},{... | collective-permute-start | bytes 18440 | tf_op jit(solution)/shard_map/ppermute | solution.py:21
  243.5 4.7 %collective-permute-start.21 = (f32[3,4,1,128]{3,2,1,0:T(1,128)S(1)}, f32[3,4,1,128]{3,2,1,0:T(1,128)S(1)}, u32[]{:S(2)}, u32[]{:S(2)}) collective-permute-start(f32[3,4,1,128]{3,2,1,0:T(1,128)S(1)} %pad_maximum_fusion.73), channel_id=1, source_target_pairs={{0,1},{1,2},{2,3},{4,5},{5,6},{6,7},{8,9},{9,10},{10,11},{12,13},{... | collective-permute-start | bytes 18440 | tf_op jit(solution)/shard_map/ppermute | solution.py:21
  248.3 3.1 collective-permute-start.24
  251.4 5.8 %collective-permute-start.25 = (f32[3,5,1,128]{3,2,1,0:T(1,128)S(1)}, f32[3,5,1,128]{3,2,1,0:T(1,128)S(1)}, u32[]{:S(2)}, u32[]{:S(2)}) collective-permute-start(f32[3,5,1,128]{3,2,1,0:T(1,128)S(1)} %pad_maximum_fusion.68), channel_id=1, source_target_pairs={{1,0},{2,1},{3,2},{5,4},{6,5},{7,6},{9,8},{10,9},{11,10},{13,12},{... | collective-permute-start | bytes 23048 | tf_op jit(solution)/shard_map/ppermute | solution.py:21
  259.3 4.3 %collective-permute-start.26 = (f32[3,1,17,128]{3,2,1,0:T(8,128)S(1)}, f32[3,1,17,128]{3,2,1,0:T(8,128)S(1)}, u32[]{:S(2)}, u32[]{:S(2)}) collective-permute-start(f32[3,1,17,128]{3,2,1,0:T(8,128)S(1)} %slice.739), channel_id=1, source_target_pairs={{0,4},{4,8},{8,12},{12,16},{16,20},{20,24},{24,28},{28,32},{32,36}... | collective-permute-start | bytes 78344 | tf_op jit(solution)/shard_map/ppermute | solution.py:21
  263.6 5.0 %collective-permute-start.27 = (f32[3,4,1,128]{3,2,1,0:T(1,128)S(1)}, f32[3,4,1,128]{3,2,1,0:T(1,128)S(1)}, u32[]{:S(2)}, u32[]{:S(2)}) collective-permute-start(f32[3,4,1,128]{3,2,1,0:T(1,128)S(1)} %pad_maximum_fusion.71), channel_id=1, source_target_pairs={{0,1},{1,2},{2,3},{4,5},{5,6},{6,7},{8,9},{9,10},{10,11},{12,13},{... | collective-permute-start | bytes 18440 | tf_op jit(solution)/shard_map/ppermute | solution.py:21
  297.3 3.1 collective-permute-start.28
  300.4 5.5 %collective-permute-start.29 = (f32[3,5,1,128]{3,2,1,0:T(1,128)S(1)}, f32[3,5,1,128]{3,2,1,0:T(1,128)S(1)}, u32[]{:S(2)}, u32[]{:S(2)}) collective-permute-start(f32[3,5,1,128]{3,2,1,0:T(1,128)S(1)} %pad_maximum_fusion.67), channel_id=1, source_target_pairs={{1,0},{2,1},{3,2},{5,4},{6,5},{7,6},{9,8},{10,9},{11,10},{13,12},{... | collective-permute-start | bytes 23048 | tf_op jit(solution)/shard_map/ppermute | solution.py:21
  308.0 3.2 collective-permute-start.30
  311.3 3.8 %collective-permute-start.31 = (f32[3,4,1,128]{3,2,1,0:T(1,128)S(1)}, f32[3,4,1,128]{3,2,1,0:T(1,128)S(1)}, u32[]{:S(2)}, u32[]{:S(2)}) collective-permute-start(f32[3,4,1,128]{3,2,1,0:T(1,128)S(1)} %pad_maximum_fusion.70), channel_id=1, source_target_pairs={{0,1},{1,2},{2,3},{4,5},{5,6},{6,7},{8,9},{9,10},{10,11},{12,13},{... | collective-permute-start | bytes 18440 | tf_op jit(solution)/shard_map/ppermute | solution.py:21
where the time goes:
time: 347 us; the launch traced here: 343 us
  other arithmetic  97 us (28%)
  starting transfers between devices  88 us (25%)
  blocking collectives  56.9 us (16%)
  local copies, waits for them, and re-layouts  55.8 us (16%)
  waiting for transfers between devices  32 us (9%)
  between operations  7.89 us (2%)
  matrix products  5.82 us (2%)
    gather x1, local copies, waits for them, and re-layouts, local(): strain_cells = jnp.take(strain, hosts).reshape(shape)  45.5 us
    all_to_all x2, blocking collectives, from_everyone(): return lax.all_to_all(copies, axis, split_axis=0, concat_axis=0, tiled=True)  44.9 us
    scatter-add x1, other arithmetic, local(): jax.ops.segment_sum(jnp.broadcast_to(flow_keep, change.shape), hosts, num...  43.2 us
    scatter-add x1, other arithmetic, local(): sums = jax.ops.segment_sum(change, hosts, num_segments=elements)  43.2 us
    ppermute x14, starting transfers between devices, passed_along(): lax.ppermute(value, axis, [(source, source + steps) for source in range(l...  33.2 us
    ppermute x9, starting transfers between devices, padded_2(): lax.ppermute(last, axis, up)  26.8 us
    ppermute x14, waiting for transfers between devices, passed_along(): lax.ppermute(value, axis, [(source, source + steps) for source in range(l...  23.9 us
    ppermute x9, starting transfers between devices, padded_2(): lax.ppermute(leading, axis, [(b, a) for a, b in up])  21.4 us
  transfers between devices with their start and end apart: 33, of which 14 were waited for; matrix products, arithmetic and copies ran while one was open for 15% of the time, Pallas kernels for 0%

commit v1 on v0

v1 whole, which is shorter than its diff:
```python
import functools

import jax
import jax.numpy as jnp
from jax import lax
from jax.experimental import pallas as pl
from jax.experimental.pallas import tpu as pltpu
from jax.sharding import PartitionSpec as P

F32 = jnp.float32
BF16 = jnp.bfloat16
I32 = jnp.int32
MESH = pl.DeviceIdType.MESH
NBLK = 64
LANES = 128
ROWS = 64
BIOT = 1.5
RELAX = 0.8
SPRING = 0.5
WELL = 4.0
AROUND = [(dx, dy) for dx in (-1, 0, 1) for dy in (-1, 0, 1) if (dx, dy) != (0, 0)]

SEND = dict(ux=3, strain=3, ue=8, ce=8, mw=8, gr=8, sums=1, counts=1, halo=18, ary=4, arx=16)
RECV = dict(ux=3, strain=1, ue=8, ce=8, mw=8, gr=8, sums=3, counts=3, halo=18, ary=4, arx=16)


def offsets(table):
    at, out = 0, {}
    for name, count in table.items():
        out[name] = at
        at += count
    return out, at


SEND_AT, N_SEND = offsets(SEND)
RECV_AT, N_RECV = offsets(RECV)

SCRATCH = dict(
    pres=((64, 128), F32), srcs=((64, 128), F32), stor=((64, 128), F32), well=((64, 128), I32),
    blk=((64, 128), I32), bas=((512, 128), F32), host=((64, 128), I32),
    disp=((3, 64, 128), F32), body=((192, 128), F32), modl=((64, 128), F32), mask=((64, 128), I32),
    stif=((24, 24), F32),
    p1=((64, 128), F32), p2=((64, 128), F32), diag=((64, 128), F32), frc=((64, 128), F32),
    xh=((6, 16, 128), F32), yh=((6, 8, 128), F32), zh=((6, 8, 128), F32),
    ys=((6, 8, 128), F32), zs=((6, 8, 128), F32),
    sti=((64, 128), F32), ol=((128, 8192), BF16), oh=((64, 8192), BF16), ob=((64, 8192), BF16),
    wt=((64, 8, 128), F32), wr=((16, 8192), BF16), ar=((128, 8192), BF16), scale=((8, 64), F32),
    rowi=((64, 128), F32), chg=((64, 128), F32), lo=((64, 128), F32), t2=((128, 128), BF16),
    cnt=((64, 128), F32), sm=((64, 128), F32), corr=((16, 64), BF16), rem=((64, 128), F32),
    ux=((3, 16, 128), F32), uy=((16, 128), F32), uc=((8, 128), F32),
    uys=((16, 128), F32), ucs=((8, 128), F32), stro=((64, 128), F32),
    ue=((8, 96, 128), F32), uyl=((8, 16, 128), F32), uyh=((8, 16, 128), F32),
    ce=((8, 96, 128), F32), cyl=((8, 16, 128), F32), cyh=((8, 16, 128), F32),
    mw=((9, 32, 128), F32), gr=((9, 32, 128), F32), wtile=((7, 88, 128), F32),
    sr=((3, 64, 128), F32), cr=((3, 64, 128), F32), fac=((64, 128), F32),
    gt=((9, 104, 128), F32), rx=((8, 96, 128), F32), qe=((8, 96, 128), F32),
    ph=((8, 192, 128), BF16), plo=((8, 192, 128), BF16), vs=((7, 704, 128), F32),
    kl=((64, 192), BF16), kap=((8, 128), F32), bt=((4, 64, 128), F32),
    rr=((192, 128), F32), qr=((192, 128), F32), dots=((8, 128), F32),
    ar1=((4, 8, 128), F32), ar2=((16, 1, 128), F32), row=((1, 128), F32),
)


def split(value):
    high = value.astype(BF16)
    return high, (value - high.astype(F32)).astype(BF16)


def dot_nt(a, b):
    return lax.dot_general(a, b, (((1,), (1,)), ((), ())), preferred_element_type=F32)


def dot_nn(a, b):
    return jnp.dot(a, b, preferred_element_type=F32)


def lane_iota(shape=(8, 128)):
    return lax.broadcasted_iota(I32, shape, len(shape) - 1)


def sub_iota(shape=(8, 128)):
    return lax.broadcasted_iota(I32, shape, len(shape) - 2)


def shift_down(value):
    return jnp.where(lane_iota(value.shape) == LANES - 1, 0.0, pltpu.roll(value, LANES - 1, 1))


def shift_up(value):
    return jnp.where(lane_iota(value.shape) == 0, 0.0, pltpu.roll(value, 1, 1))


def loop(count, body, unroll=1):
    def step(i, carry):
        body(i)
        return carry

    lax.fori_loop(0, count, step, 0, unroll=unroll)


def kernel(sizes, *refs):
    groups, nx, ny = sizes
    ins, (po, do), rest = refs[:12], refs[12:14], refs[14:]
    s = dict(zip(SCRATCH, rest))
    in_sems, send_sems, recv_sems, known = rest[len(SCRATCH):]
    g, gx, gy = lax.axis_index("grp"), lax.axis_index("gx"), lax.axis_index("gy")
    top = groups - 1
    mech = g == top
    names = ["pres", "srcs", "stor", "well", "blk", "bas", "host", "disp", "body", "modl", "mask", "stif"]

    def local(name):
        k = names.index(name)
        return pltpu.make_async_copy(ins[k], s[name], in_sems.at[k])

    def inside(dx, dy, dg=0):
        x, y = gx + dx, gy + dy
        ok = (x >= 0) & (x < nx) & (y >= 0) & (y < ny)
        if dg:
            ok = ok & (g + dg >= 0) & (g + dg < top)
        return ok

    def as_int(flag):
        return flag.astype(I32)

    def remote(src, dst, send, recv, device):
        return pltpu.make_async_remote_copy(
            src_ref=src, dst_ref=dst, send_sem=send_sems.at[send], recv_sem=recv_sems.at[recv],
            device_id=device, device_id_type=MESH,
        )

    def start_if(ok, *args):
        @pl.when(ok)
        def _():
            remote(*args).start()

    def wait_recv_if(ok, dst, recv):
        @pl.when(ok)
        def _():
            remote(dst, dst, 0, recv, (g, gx, gy)).wait_recv()

    def wait_send_if(ok, src, send):
        @pl.when(ok)
        def _():
            remote(src, src, send, 0, (g, gx, gy)).wait_send()

    def greet(ok, device):
        @pl.when(ok)
        def _():
            pl.semaphore_signal(pltpu.get_barrier_semaphore(), inc=1, device_id=device, device_id_type=MESH)

    HALO = [(-1, 0, 0), (1, 0, 0), (0, -1, 0), (0, 1, 0), (0, 0, -1), (0, 0, 1)]

    def halo_refs(p, k, way):
        dx, dy, dg = HALO[way]
        if dx:
            src = p.at[0:16] if dx < 0 else p.at[48:64]
            return src, s["xh"].at[2 * k + (1 if dx < 0 else 0)]
        if dy:
            return s["ys"].at[2 * k + (0 if dy < 0 else 1)], s["yh"].at[2 * k + (1 if dy < 0 else 0)]
        return s["zs"].at[2 * k + (0 if dg < 0 else 1)], s["zh"].at[2 * k + (1 if dg < 0 else 0)]

    def stage_halos(p, k):
        lane = lane_iota()
        low = jnp.zeros((8, 128), F32)
        high = jnp.zeros((8, 128), F32)
        for v in range(8):
            tile = p[8 * v : 8 * v + 8]
            low = jnp.where(lane == v, tile if v == 0 else pltpu.roll(tile, v, 1), low)
            high = jnp.where(lane == v, pltpu.roll(tile, v + 1, 1), high)
        s["zs"][2 * k] = low
        s["zs"][2 * k + 1] = high
        for x in range(4):
            s["ys"][2 * k, x : x + 1] = p[16 * x : 16 * x + 1]
            s["ys"][2 * k + 1, x : x + 1] = p[16 * x + 15 : 16 * x + 16]

    def send_halos(p, k):
        for way, (dx, dy, dg) in enumerate(HALO):
            src, dst = halo_refs(p, k, way)
            sem = 6 * k + way
            start_if(inside(dx, dy, dg), src, dst, SEND_AT["halo"] + sem, RECV_AT["halo"] + sem, (g + dg, gx + dx, gy + dy))

    def wait_halos(p, k):
        for way, (dx, dy, dg) in enumerate(HALO):
            _, dst = halo_refs(p, k, way)
            wait_recv_if(inside(-dx, -dy, -dg), dst, RECV_AT["halo"] + 6 * k + way)

    def around(p, k):
        lane = lane_iota()
        value = p[...]
        xlo, xhi = s["xh"][2 * k], s["xh"][2 * k + 1]
        total = jnp.concatenate([xlo, value[:48]], 0) + jnp.concatenate([value[16:], xhi], 0)
        ylo = jnp.concatenate([jnp.broadcast_to(s["yh"][2 * k, x : x + 1], (16, 128)) for x in range(4)], 0)
        yhi = jnp.concatenate([jnp.broadcast_to(s["yh"][2 * k + 1, x : x + 1], (16, 128)) for x in range(4)], 0)
        row = lax.rem(sub_iota((64, 128)), 16)
        total = total + jnp.where(row == 0, ylo, pltpu.roll(value, 1, 0))
        total = total + jnp.where(row == 15, yhi, pltpu.roll(value, 63, 0))
        zlo, zhi = s["zh"][2 * k], s["zh"][2 * k + 1]
        parts = []
        for v in range(8):
            tile = value[8 * v : 8 * v + 8]
            below = zlo if v == 0 else pltpu.roll(zlo, LANES - v, 1)
            above = pltpu.roll(zhi, LANES - 1 - v, 1)
            parts.append(
                jnp.where(lane == 0, below, pltpu.roll(tile, 1, 1))
                + jnp.where(lane == LANES - 1, above, pltpu.roll(tile, LANES - 1, 1))
            )
        return total + jnp.concatenate(parts, 0)

    def cols(i, width=1024):
        return pl.ds(pl.multiple_of(i * width, width), width)

    def rows8(i):
        return pl.ds(pl.multiple_of(i * 8, 8), 8)

    def flow():
        for name in ("pres", "host", "stor", "well", "srcs", "blk", "bas"):
            local(name).start()
        for name in ("xh", "yh", "zh"):
            s[name][...] = jnp.zeros(SCRATCH[name][0], F32)
        count = I32(1)
        greet(gx >= 0, (top, gx, gy))
        for dx, dy, dg in HALO:
            greet(inside(dx, dy, dg), (g + dg, gx + dx, gy + dy))
            count = count + as_int(inside(dx, dy, dg))
        local("pres").wait()
        stage_halos(s["pres"], 0)
        pl.semaphore_wait(pltpu.get_barrier_semaphore(), count)
        send_halos(s["pres"], 0)

        local("host").wait()
        iota_l = sub_iota((128, 128))
        iota_r = sub_iota((64, 128))

        def hosts(i):
            index = s["host"][rows8(i)]
            lanes, rows = index & 127, index >> 7
            s["rowi"][rows8(i)] = rows.astype(F32)
            left, right = [], []
            for r in range(8):
                left.append((iota_l == lanes[r : r + 1]).astype(F32).astype(BF16))
                right.append((iota_r == rows[r : r + 1]).astype(F32).astype(BF16))
            s["ol"][:, cols(i)] = jnp.concatenate(left, 1)
            s["oh"][:, cols(i)] = jnp.concatenate(right, 1)

        loop(8, hosts)
        for name in ("stor", "well", "srcs", "blk", "bas"):
            local(name).wait()
        s["diag"][...] = 6.0 + s["stor"][...] + WELL * s["well"][...].astype(F32)

        def blocks(i):
            index = s["blk"][rows8(i)]
            diag = s["diag"][rows8(i)]
            parts, highs, lows = [], [], []
            for r in range(8):
                parts.append((iota_r == index[r : r + 1]).astype(F32).astype(BF16))
                weight = s["bas"][pl.ds(i * 8 + r, 8, stride=64), :]
                s["wt"][i * 8 + r] = weight
                term = weight * weight * diag[r : r + 1]
                high = term.astype(BF16).astype(F32)
                highs.append(jnp.concatenate([high, term - high], 0).astype(BF16))
            s["ob"][:, cols(i)] = jnp.concatenate(parts, 1)
            s["wr"][:, cols(i)] = jnp.concatenate(highs, 1)

        loop(8, blocks)
        wait_recv_if(gx >= 0, s["sti"], RECV_AT["strain"])
        high, low = split(s["sti"][...])
        s["t2"][0:64] = high
        s["t2"][64:128] = low

        iota_f = iota_r.astype(F32)

        def gather(i):
            table = dot_nn(s["t2"][...], s["ol"][:, cols(i)])
            rows = s["rowi"][rows8(i)]
            parts = []
            for r in range(8):
                column = table[0:64, 128 * r : 128 * r + 128] + table[64:128, 128 * r : 128 * r + 128]
                parts.append(jnp.sum(jnp.where(iota_f == rows[r : r + 1], column, 0.0), axis=0, keepdims=True))
            s["frc"][rows8(i)] = s["srcs"][rows8(i)] - BIOT * jnp.concatenate(parts, 0)

        loop(8, gather)

        def residual(p, k):
            return s["frc"][...] + around(p, k) - s["diag"][...] * p[...]

        wait_halos(s["pres"], 0)
        s["p1"][...] = s["pres"][...] + RELAX * residual(s["pres"], 0) / s["diag"][...]
        stage_halos(s["p1"], 1)
        send_halos(s["p1"], 1)
        norms = dot_nt(s["wr"][...], s["ob"][...])
        s["scale"][...] = 1.0 + norms[0:8] + norms[8:16]
        wait_halos(s["p1"], 1)
        s["p2"][...] = s["p1"][...] + RELAX * residual(s["p1"], 1) / s["diag"][...]
        stage_halos(s["p2"], 2)
        send_halos(s["p2"], 2)
        s["cnt"][...] = dot_nt(s["oh"][...], s["ol"][...])
        start_if(gx >= 0, s["cnt"], s["cr"].at[g], SEND_AT["counts"], RECV_AT["counts"] + g, (top, gx, gy))
        wait_halos(s["p2"], 2)
        s["rem"][...] = residual(s["p2"], 2)

        def weighted(i):
            rem = s["rem"][rows8(i)]
            highs = []
            for r in range(8):
                term = s["wt"][i * 8 + r] * rem[r : r + 1]
                high = term.astype(BF16).astype(F32)
                highs.append(jnp.concatenate([high, term - high], 0).astype(BF16))
            s["wr"][:, cols(i)] = jnp.concatenate(highs, 1)

        loop(8, weighted)
        coarse = dot_nt(s["wr"][...], s["ob"][...])
        fixed = (coarse[0:8] + coarse[8:16]) / s["scale"][...]
        high = fixed.astype(BF16).astype(F32)
        s["corr"][...] = jnp.concatenate([high, fixed - high], 0).astype(BF16)

        def spread_back(i):
            back = dot_nn(s["corr"][...], s["ob"][:, cols(i)])
            back = back[0:8] + back[8:16]
            parts = []
            for r in range(8):
                parts.append(jnp.sum(s["wt"][i * 8 + r] * back[:, 128 * r : 128 * r + 128], axis=0, keepdims=True))
            updated = s["p2"][rows8(i)] + jnp.concatenate(parts, 0)
            po[rows8(i)] = updated
            change = updated - s["pres"][rows8(i)]
            high = change.astype(BF16).astype(F32)
            low = change - high
            tops, lows = [], []
            for r in range(8):
                one = s["oh"][:, pl.ds(pl.multiple_of(i * 1024 + 128 * r, 128), 128)]
                tops.append(one * jnp.broadcast_to(high[r : r + 1], (64, 128)).astype(BF16))
                lows.append(one * jnp.broadcast_to(low[r : r + 1], (64, 128)).astype(BF16))
            s["ar"][0:64, cols(i)] = jnp.concatenate(tops, 1)
            s["ar"][64:128, cols(i)] = jnp.concatenate(lows, 1)

        loop(8, spread_back)
        both = dot_nt(s["ar"][...], s["ol"][...])
        s["sm"][...] = both[0:64] + both[64:128]
        start_if(gx >= 0, s["sm"], s["sr"].at[g], SEND_AT["sums"], RECV_AT["sums"] + g, (top, gx, gy))
        do[...] = jnp.zeros((192, 128), F32)
        for k, p in enumerate((s["pres"], s["p1"], s["p2"])):
            for way, (dx, dy, dg) in enumerate(HALO):
                src, _ = halo_refs(p, k, way)
                wait_send_if(inside(dx, dy, dg), src, SEND_AT["halo"] + 6 * k + way)
        wait_send_if(gx >= 0, s["cnt"], SEND_AT["counts"])
        wait_send_if(gx >= 0, s["sm"], SEND_AT["sums"])

    def x_from(dx, low, high):
        first = low
        if dx == 0:
            return slice(first, first + 4), slice(first, first + 4)
        if dx < 0:
            return slice(first, first + high), slice(first + 4, first + 4 + high)
        return slice(first + 4 - low, first + 4), slice(0, low)

    def node_refs(arr, ylo, yhi, dx, dy):
        xs, xd = x_from(dx, 2, 2)
        if dy == 0:
            return arr.at[xs, 16:80], arr.at[xd, 16:80]
        if dy > 0:
            return arr.at[xs, 64:80], ylo.at[xd]
        return arr.at[xs, 16:32], yhi.at[xd]

    def raw_refs(arr, dx, dy):
        xs, xd = x_from(dx, 3, 2)
        ysrc, ydst = {0: (slice(8, 24), slice(8, 24)), 1: (slice(16, 24), slice(0, 8)), -1: (slice(8, 16), slice(24, 32))}[dy]
        return arr.at[xs, ysrc], arr.at[xd, ydst]

    def exchange_start(refs_of, name):
        for k, (dx, dy) in enumerate(AROUND):
            src, dst = refs_of(dx, dy)
            start_if(inside(dx, dy), src, dst, SEND_AT[name] + k, RECV_AT[name] + k, (g, gx + dx, gy + dy))

    def exchange_wait(refs_of, name):
        for k, (dx, dy) in enumerate(AROUND):
            _, dst = refs_of(dx, dy)
            wait_recv_if(inside(-dx, -dy), dst, RECV_AT[name] + k)

    def exchange_done(refs_of, name):
        for k, (dx, dy) in enumerate(AROUND):
            src, _ = refs_of(dx, dy)
            wait_send_if(inside(dx, dy), src, SEND_AT[name] + k)

    def close_nodes(arr, ylo, yhi):
        half = sub_iota() < 4

        def plane(x):
            for k in range(2):
                own = arr[x, 64 + 8 * k : 72 + 8 * k]
                arr[x, 8 * k : 8 * k + 8] = pltpu.roll(jnp.where(half, own, ylo[x, 8 * k : 8 * k + 8]), 4, 0)
                own = arr[x, 16 + 8 * k : 24 + 8 * k]
                arr[x, 80 + 8 * k : 88 + 8 * k] = pltpu.roll(jnp.where(half, yhi[x, 8 * k : 8 * k + 8], own), 4, 0)

        loop(8, plane)

    def zero_edges(arr, ylo, yhi):
        @pl.when(gx == 0)
        def _():
            arr[0:2] = jnp.zeros((2,) + arr.shape[1:], F32)
            ylo[0:2] = jnp.zeros((2, 16, 128), F32)
            yhi[0:2] = jnp.zeros((2, 16, 128), F32)

        @pl.when(gx == nx - 1)
        def _():
            arr[6:8] = jnp.zeros((2,) + arr.shape[1:], F32)
            ylo[6:8] = jnp.zeros((2, 16, 128), F32)
            yhi[6:8] = jnp.zeros((2, 16, 128), F32)

        @pl.when(gy == 0)
        def _():
            ylo[...] = jnp.zeros((8, 16, 128), F32)

        @pl.when(gy == ny - 1)
        def _():
            yhi[...] = jnp.zeros((8, 16, 128), F32)

    def zero_raw(arr):
        @pl.when(gx == 0)
        def _():
            arr[0:3] = jnp.zeros((3, 32, 128), F32)

        @pl.when(gx == nx - 1)
        def _():
            arr[7:9] = jnp.zeros((2, 32, 128), F32)

        @pl.when(gy == 0)
        def _():
            arr[:, 0:8] = jnp.zeros((9, 8, 128), F32)

        @pl.when(gy == ny - 1)
        def _():
            arr[:, 24:32] = jnp.zeros((9, 8, 128), F32)

    def x_ok(x):
        bad = ((x < 2) & (gx == 0)) | ((x >= 6) & (gx == nx - 1))
        return jnp.where(bad, 0.0, 1.0).astype(F32)

    def y_ok(j):
        sub = sub_iota()
        mask = jnp.where((sub & 3) < 3, 1.0, 0.0)
        if j < 2:
            mask = jnp.where(sub < 4, mask * jnp.where(gy == 0, 0.0, 1.0), mask)
        if j > 9:
            mask = jnp.where(sub >= 4, mask * jnp.where(gy == ny - 1, 0.0, 1.0), mask)
        return mask

    def operate(arr, elem_x, elem_j, use):
        (xa, xb), (ja, jb) = elem_x, elem_j
        ph, plo, vs = s["ph"], s["plo"], s["vs"]
        wide = jb - ja

        def stage(k):
            x = xa + k
            for j in range(ja, jb + 1):
                value = arr[x, 8 * j : 8 * j + 8]
                pair = jnp.concatenate([value, shift_down(value)], 0)
                high, low = split(pair)
                ph[x, 16 * j : 16 * j + 16] = high
                plo[x, 16 * j : 16 * j + 16] = low

        loop(xb - xa + 1, stage)

        def elements(k):
            x = xa + k
            columns = []
            for j in range(ja, jb):
                at = slice(16 * j, 16 * j + 32)
                first, second = ph[x, at], ph[x + 1, at]
                columns.append(jnp.concatenate([first, second, plo[x, at], plo[x + 1, at], first, second], 0))
            product = dot_nn(s["kl"][...], jnp.concatenate(columns, 1))
            for c in range(wide):
                j = ja + c
                weight = s["wtile"][x, 8 * j : 8 * j + 8]
                vs[x, 64 * j : 64 * j + 64] = product[:, 128 * c : 128 * c + 128] * jnp.concatenate([weight] * 8, 0)

        loop(xb - xa, elements)

        spring = SPRING * s["kap"][...]

        def nodes(k):
            x = xa + 1 + k
            for j in range(ja + 1, jb):
                total = None
                for a in range(2):
                    for b in range(2):
                        at = 64 * (j - b) + 16 * (2 * a + b)
                        part = vs[x - a, at : at + 16]
                        total = part if total is None else total + part
                node = arr[x, 8 * j : 8 * j + 8]
                use(x, j, node, total[0:8] + shift_up(total[8:16]) + spring * node)

        loop(xb - xa - 1, nodes)

    def mechanics():
        for name in ("disp", "mask", "modl", "stif", "body"):
            local(name).start()
        greet_count = I32(top)
        for gg in range(top):
            greet(gx >= 0, (gg, gx, gy))
        for dx, dy in AROUND:
            greet(inside(dx, dy), (g, gx + dx, gy + dy))
            greet_count = greet_count + as_int(inside(dx, dy))
        local("disp").wait()
        disp = s["disp"]
        for m in range(3):
            for x in range(4):
                s["uys"][4 * m + x : 4 * m + x + 1] = disp[m, 16 * x : 16 * x + 1]
            s["ucs"][m : m + 1] = disp[m, 0:1]
        pl.semaphore_wait(pltpu.get_barrier_semaphore(), greet_count)

        near = [
            (-1, 0, disp.at[:, 0:16], s["ux"]),
            (0, -1, s["uys"], s["uy"]),
            (-1, -1, s["ucs"], s["uc"]),
        ]
        for k, (dx, dy, src, dst) in enumerate(near):
            start_if(inside(dx, dy), src, dst, SEND_AT["ux"] + k, RECV_AT["ux"] + k, (g, gx + dx, gy + dy))

        @pl.when(gx == nx - 1)
        def _():
            s["ux"][...] = jnp.zeros((3, 16, 128), F32)
            s["uc"][...] = jnp.zeros((8, 128), F32)

        @pl.when(gy == ny - 1)
        def _():
            s["uy"][...] = jnp.zeros((16, 128), F32)
            s["uc"][...] = jnp.zeros((8, 128), F32)

        local("mask").wait()
        for k, (dx, dy, _, dst) in enumerate(near):
            wait_recv_if(inside(-dx, -dy), dst, RECV_AT["ux"] + k)

        row15 = sub_iota((16, 128)) == 15
        before = None
        for x in range(5):
            sums, diffs = [], []
            for m in range(3):
                plane = disp[m, 16 * x : 16 * x + 16] if x < 4 else s["ux"][m]
                beyond = s["uy"][4 * m + x : 4 * m + x + 1] if x < 4 else s["uc"][m : m + 1]
                up = jnp.where(row15, jnp.broadcast_to(beyond, (16, 128)), pltpu.roll(plane, 15, 0))
                sums.append(up + plane)
                diffs.append(up - plane)
            now = (sums[0], diffs[1], sums[2])
            if before is not None:
                plain = (now[0] - before[0]) + (now[1] + before[1])
                third = now[2] + before[2]
                value = (plain - third) + shift_down(plain + third)
                at = 16 * (x - 1)
                s["stro"][at : at + 16] = 0.25 * s["mask"][at : at + 16].astype(F32) * value
            before = now
        for gg in range(top):
            start_if(gx >= 0, s["stro"], s["sti"], SEND_AT["strain"] + gg, RECV_AT["strain"], (gg, gx, gy))

        ue, ce = s["ue"], s["ce"]
        local("modl").wait()
        local("body").wait()
        local("stif").wait()
        zero = jnp.zeros((64, 128), F32)
        for x in range(4):
            ue[x + 2, 16:80] = zero
            s["bt"][x] = zero
            for m in range(3):
                for h in range(2):
                    at = 16 * x + 8 * h
                    ue[x + 2, pl.ds(16 + 4 * h + m, 8, stride=8), :] = disp[m, at : at + 8]
                    at = 64 * m + at
                    s["bt"][x, pl.ds(4 * h + m, 8, stride=8), :] = s["body"][at : at + 8]
            at = 16 * x
            s["mw"][x + 3, 8:24] = s["modl"][at : at + 16] * s["mask"][at : at + 16].astype(F32)
        ue_refs = functools.partial(node_refs, ue, s["uyl"], s["uyh"])
        ce_refs = functools.partial(node_refs, ce, s["cyl"], s["cyh"])
        mw_refs = functools.partial(raw_refs, s["mw"])
        gr_refs = functools.partial(raw_refs, s["gr"])
        exchange_start(ue_refs, "ue")
        exchange_start(mw_refs, "mw")
        zero_edges(ue, s["uyl"], s["uyh"])
        zero_edges(ce, s["cyl"], s["cyh"])
        zero_raw(s["mw"])
        zero_raw(s["gr"])

        stiff = s["stif"][...]
        largest = jnp.max(jnp.max(jnp.abs(stiff), axis=1, keepdims=True), axis=0, keepdims=True)
        s["kap"][...] = jnp.broadcast_to(1.0 / largest, (8, 128))
        high, low = split(stiff / largest)
        line = lax.broadcasted_iota(I32, (64, 24), 0)
        entry = lax.broadcasted_iota(I32, (64, 24), 1)
        pick = jnp.where(((line & 3) < 3) & (3 * (line >> 3) + (line & 3) == entry), 1.0, 0.0).astype(BF16)
        r_half = (lax.broadcasted_iota(I32, (64, 64), 0) >> 2) & 1
        c_half = (lax.broadcasted_iota(I32, (64, 64), 1) >> 2) & 1
        wide = []
        for part in (high, low):
            rows = dot_nn(pick, part).astype(BF16)
            wide.append(jnp.where(r_half == c_half, dot_nt(rows, pick), 0.0).astype(BF16))
        s["kl"][...] = jnp.concatenate([wide[0], wide[0], wide[1]], 1)

        step, turn = 1, 0
        for size, coord, axis in ((nx, gx, 1), (ny, gy, 2)):
            step = 1
            while step < size:
                back, ahead = coord - step >= 0, coord + step < size
                for ok, move in ((back, -step), (ahead, step)):
                    device = (g, gx + move, gy) if axis == 1 else (g, gx, gy + move)

                    @pl.when(ok)
                    def _():
                        pl.semaphore_signal(known.at[turn], inc=1, device_id=device, device_id_type=MESH)

                pl.semaphore_wait(known.at[turn], as_int(back) + as_int(ahead))
                step, turn = step * 2, turn + 1

        exchange_wait(mw_refs, "mw")
        half = sub_iota() < 4

        def pair_of_rows(arr, x, low):
            return jnp.where(
                half,
                jnp.broadcast_to(arr[x, low : low + 1], (8, 128)),
                jnp.broadcast_to(arr[x, low + 8 : low + 9], (8, 128)),
            )

        def weights(x):
            for j in range(11):
                s["wtile"][x, 8 * j : 8 * j + 8] = pair_of_rows(s["mw"], x + 1, 6 + j)

        loop(7, weights)
        exchange_wait(ue_refs, "ue")
        close_nodes(ue, s["uyl"], s["uyh"])
        kappa = jnp.broadcast_to(largest, (8, 128))

        def initial(x, j, node, product):
            ce[x, 8 * j : 8 * j + 8] = s["bt"][x - 2, 8 * (j - 2) : 8 * (j - 2) + 8] - kappa * product

        operate(ue, (1, 6), (1, 10), initial)
        exchange_start(ce_refs, "ce")
        exchange_wait(ce_refs, "ce")
        close_nodes(ce, s["cyl"], s["cyh"])

        for gg in range(top):
            wait_recv_if(gx >= 0, s["cr"].at[gg], RECV_AT["counts"] + gg)
        counts = s["cr"][0]
        for gg in range(1, top):
            counts = counts + s["cr"][gg]
        s["fac"][...] = (0.25 * BIOT) * s["mask"][...].astype(F32) / jnp.maximum(counts, 1.0)
        po[...] = jnp.zeros((64, 128), F32)

        for gg in range(top):
            wait_recv_if(gx >= 0, s["sr"].at[gg], RECV_AT["sums"] + gg)
        sums = s["sr"][0]
        for gg in range(1, top):
            sums = sums + s["sr"][gg]
        value = s["fac"][...] * sums
        for x in range(4):
            s["gr"][x + 3, 8:24] = value[16 * x : 16 * x + 16]
        exchange_start(gr_refs, "gr")
        exchange_wait(gr_refs, "gr")

        def tiles(x):
            for j in range(13):
                s["gt"][x, 8 * j : 8 * j + 8] = pair_of_rows(s["gr"], x, 5 + j)

        loop(9, tiles)
        part = sub_iota() & 3
        signs = [jnp.where(part == m, -1.0, 1.0).astype(F32) for m in range(3)]
        rx, qe = s["rx"], s["qe"]

        def force(x):
            okay = x_ok(x)
            last = None
            for j in range(13):
                at = slice(8 * j, 8 * j + 8)
                along_x = s["gt"][x, at] + signs[0] * s["gt"][x + 1, at]
                if last is not None:
                    both = last + signs[1] * along_x
                    node = shift_up(both) + signs[2] * both
                    k = j - 1
                    at = slice(8 * k, 8 * k + 8)
                    rx[x, at] = (ce[x, at] + node) * (y_ok(k) * okay)
                last = along_x

        loop(8, force)

        def first(x, j, node, product):
            qe[x, 8 * j : 8 * j + 8] = product * (y_ok(j) * x_ok(x))

        operate(rx, (0, 7), (0, 11), first)
        acc = s["dots"]
        acc[...] = jnp.zeros((8, 128), F32)

        def second(x, j, node, product):
            r = rx[x, 8 * j : 8 * j + 8]
            terms = [r * r, r * node, node * node, node * product]
            rows = [jnp.sum(term, axis=0, keepdims=True) for term in terms]
            acc[0:4] += jnp.concatenate(rows, 0)

        operate(qe, (1, 6), (1, 10), second)
        ar1, ar2 = s["ar1"], s["ar2"]
        for d in range(1, ny):
            start_if(gx >= 0, acc, ar1.at[d], SEND_AT["ary"] + d, RECV_AT["ary"] + d, (g, gx, lax.rem(gy + d, ny)))

        def to_rows(arr, out):
            for x in range(4):
                for m in range(3):
                    for h in range(2):
                        at = 64 * m + 16 * x + 8 * h
                        out[at : at + 8] = arr[x + 2, pl.ds(16 + 4 * h + m, 8, stride=8), :]

        to_rows(rx, s["rr"])
        total = acc[...]
        for d in range(1, ny):
            wait_recv_if(gx >= 0, ar1.at[d], RECV_AT["ary"] + d)
            total = total + ar1[d]
        total = jnp.broadcast_to(jnp.sum(total, axis=1, keepdims=True), (8, 128))
        s["row"][...] = jnp.sum(jnp.where(lane_iota() == sub_iota(), total, 0.0), axis=0, keepdims=True)
        for d in range(1, nx):
            start_if(gx >= 0, s["row"], ar2.at[d], SEND_AT["arx"] + d, RECV_AT["arx"] + d, (g, lax.rem(gx + d, nx), gy))
        to_rows(qe, s["qr"])
        total = s["row"][...]
        for d in range(1, nx):
            wait_recv_if(gx >= 0, ar2.at[d], RECV_AT["arx"] + d)
            total = total + ar2[d]
        lane = lane_iota((1, 128))
        aa, bb, cc, ee = [
            jnp.broadcast_to(jnp.sum(jnp.where(lane == k, total, 0.0), axis=1, keepdims=True), (8, 128)) for k in range(4)
        ]
        step0 = aa / bb
        new = step0 * step0 * cc - aa
        along = bb - 2.0 * step0 * cc + step0 * step0 * ee
        ratio = new / aa
        step1 = new / (along - ratio * new / step0)
        inverse = s["kap"][...]
        alpha = (step0 + step1 * (1.0 + ratio)) * inverse
        gamma = step1 * step0 * inverse
        for k in range(24):
            at = 8 * k
            m, r = divmod(at, 64)
            do[at : at + 8] = disp[m, r : r + 8] + alpha * s["rr"][at : at + 8] - gamma * s["qr"][at : at + 8]

        for k, (dx, dy, src, _) in enumerate(near):
            wait_send_if(inside(dx, dy), src, SEND_AT["ux"] + k)
        for gg in range(top):
            wait_send_if(gx >= 0, s["stro"], SEND_AT["strain"] + gg)
        for refs_of, name in ((ue_refs, "ue"), (mw_refs, "mw"), (ce_refs, "ce"), (gr_refs, "gr")):
            exchange_done(refs_of, name)
        for d in range(1, ny):
            wait_send_if(gx >= 0, acc, SEND_AT["ary"] + d)
        for d in range(1, nx):
            wait_send_if(gx >= 0, s["row"], SEND_AT["arx"] + d)

    pl.when(jnp.logical_not(mech))(flow)
    pl.when(mech)(mechanics)


def local(sizes, *arrays):
    shapes = [(64, 128)] * 5 + [(512, 128), (64, 128), (3, 64, 128), (192, 128), (64, 128), (64, 128), (24, 24)]
    flat = [array.reshape(shape) for array, shape in zip(arrays, shapes)]
    scratch = [pltpu.VMEM(shape, dtype) for shape, dtype in SCRATCH.values()]
    scratch += [
        pltpu.SemaphoreType.DMA((12,)),
        pltpu.SemaphoreType.DMA((N_SEND,)),
        pltpu.SemaphoreType.DMA((N_RECV,)),
        pltpu.SemaphoreType.REGULAR((8,)),
    ]
    pressure, displacement = pl.pallas_call(
        functools.partial(kernel, sizes),
        out_shape=(jax.ShapeDtypeStruct((64, 128), F32), jax.ShapeDtypeStruct((192, 128), F32)),
        in_specs=[pl.BlockSpec(memory_space=pl.ANY)] * 12,
        out_specs=(pl.BlockSpec(memory_space=pltpu.VMEM),) * 2,
        scratch_shapes=scratch,
        compiler_params=pltpu.CompilerParams(collective_id=0, has_side_effects=True),
    )(*flat)
    return pressure.reshape(arrays[0].shape), displacement.reshape(arrays[7].shape)


def solution(mesh):
    cell = P("grp", "gx", "gy", None)
    many = P("grp", None, "gx", "gy", None)
    sizes = (mesh.shape["grp"], mesh.shape["gx"], mesh.shape["gy"])
    return jax.shard_map(
        functools.partial(local, sizes),
        mesh=mesh,
        in_specs=(cell,) * 5 + (many, cell, many, many, cell, cell, P()),
        out_specs=(cell, many),
        check_vma=False,
    )
```

time: 347 us -> 51.6 us (0.15)
  other arithmetic: 97 us -> 0 us
  starting transfers between devices: 88 us -> 0 us
  blocking collectives: 56.9 us -> 0 us
  local copies, waits for them, and re-layouts: 55.8 us -> 2.91 us
  Pallas kernels: 0 us -> 47.8 us
  waiting for transfers between devices: 32 us -> 0 us
  between operations: 7.89 us -> 0.64 us
  matrix products: 5.82 us -> 0 us
    scatter-add x2 -> x0, other arithmetic: 86.5 us -> none  [the longest x1 43.2 us: local(): jax.ops.segment_sum(jnp.broadcast_to(flow_keep, change.shape), hosts, num...]
    ppermute x32 -> x0, starting transfers between devices: 81.4 us -> none  [the longest x14 33.2 us: passed_along(): lax.ppermute(value, axis, [(source, source + steps) for source in range(l...]
    pallas_call x0 -> x1, Pallas kernels: none -> 47.8 us  [local(): pl.pallas_call(functools.partial(kernel, sizes), out_shape=(jax.ShapeDtyp...]
    gather x1 -> x0, local copies, waits for them, and re-layouts: 45.5 us -> none  [local(): strain_cells = jnp.take(strain, hosts).reshape(shape)]
    all_to_all x2 -> x0, blocking collectives: 44.9 us -> none  [from_everyone(): return lax.all_to_all(copies, axis, split_axis=0, concat_axis=0, tiled=True)]
    ppermute x32 -> x0, waiting for transfers between devices: 26.4 us -> none  [the longest x14 23.9 us: passed_along(): lax.ppermute(value, axis, [(source, source + steps) for source in range(l...]
    all_gather x1 -> x0, blocking collectives: 12 us -> none  [picked(): lax.all_gather(array, axis)]
    all_to_all x1 -> x0, starting transfers between devices: 6.52 us -> none  [from_everyone(): return lax.all_to_all(copies, axis, split_axis=0, concat_axis=0, tiled=True)]
  transfers between devices with their start and end apart: 33 -> 0, of which waited for: 14 -> 0; matrix products, arithmetic and copies ran while one was open for 15% -> 0% of each run, Pallas kernels for 0% -> 0%
where the time goes in v1:
time: 51.6 us; the launch traced here: 51.4 us
  Pallas kernels  47.8 us (93%)
  local copies, waits for them, and re-layouts  2.91 us (6%)
  between operations  0.64 us (1%)
    pallas_call x1, Pallas kernels, local(): pl.pallas_call(functools.partial(kernel, sizes), out_shape=(jax.ShapeDtyp...  47.8 us
    unnamed x2, local copies, waits for them, and re-layouts  2.91 us

profile of v1, /device:TPU:24, one launch (start us, length us, event | category | flops | bytes accessed | tf_op | source)
XLA Modules:
  0.0 51.4 jit_solution(13579104508610305692)
XLA Ops:
  0.6 47.8 %shard_map.131 = (f32[64,128]{1,0:T(8,128)}, f32[192,128]{1,0:T(8,128)}) custom-call(f32[64,128]{1,0:T(8,128)} %bitcast.17, f32[64,128]{1,0:T(8,128)} %bitcast.18, f32[64,128]{1,0:T(8,128)} %bitcast.19, s32[64,128]{1,0:T(8,128)} %bitcast.20, s32[64,128]{1,0:T(8,128)} %bitcast.21, f32[512,128]{1,0:T(8,128)} %bitcast.13, s32[64,128]{1,0:T(8,128)} %bitcast.22, ...), custom_call_target="tpu_custom_call" | custom-call | tf_op jit(solution)/shard_map/pallas_call | solution.py:762
  48.4 1.4 %copy.16 = f32[1,4,16,128]{3,2,1,0:T(8,128)} copy(f32[1,4,16,128]{3,2,1,0:T(8,128)} %bitcast.25) | data formatting | bytes 65536
  49.8 1.5 %copy.17 = f32[1,3,4,16,128]{4,3,2,1,0:T(8,128)} copy(f32[1,3,4,16,128]{4,3,2,1,0:T(8,128)} %bitcast.14) | data formatting | bytes 196608

commit v2 on v1

--- a/solution.py
+++ b/solution.py
@@ -44,9 +44,9 @@
     xh=((6, 16, 128), F32), yh=((6, 8, 128), F32), zh=((6, 8, 128), F32),
     ys=((6, 8, 128), F32), zs=((6, 8, 128), F32),
     sti=((64, 128), F32), ol=((128, 8192), BF16), oh=((64, 8192), BF16), ob=((64, 8192), BF16),
-    wt=((64, 8, 128), F32), wr=((16, 8192), BF16), ar=((128, 8192), BF16), scale=((8, 64), F32),
-    rowi=((64, 128), F32), chg=((64, 128), F32), lo=((64, 128), F32), t2=((128, 128), BF16),
-    cnt=((64, 128), F32), sm=((64, 128), F32), corr=((16, 64), BF16), rem=((64, 128), F32),
+    wt=((64, 8, 128), F32), wr=((16, 8192), BF16), scale=((8, 64), F32),
+    chg=((64, 128), F32), lo=((64, 128), F32),
+    cnt=((64, 128), F32), sm=((64, 128), F32), rem=((64, 128), F32),
     ux=((3, 16, 128), F32), uy=((16, 128), F32), uc=((8, 128), F32),
     uys=((16, 128), F32), ucs=((8, 128), F32), stro=((64, 128), F32),
     ue=((8, 96, 128), F32), uyl=((8, 16, 128), F32), uyh=((8, 16, 128), F32),
@@ -234,7 +234,6 @@
         def hosts(i):
             index = s["host"][rows8(i)]
             lanes, rows = index & 127, index >> 7
-            s["rowi"][rows8(i)] = rows.astype(F32)
             left, right = [], []
             for r in range(8):
                 left.append((iota_l == lanes[r : r + 1]).astype(F32).astype(BF16))
@@ -263,22 +262,16 @@
 
         loop(8, blocks)
         wait_recv_if(gx >= 0, s["sti"], RECV_AT["strain"])
-        high, low = split(s["sti"][...])
-        s["t2"][0:64] = high
-        s["t2"][64:128] = low
-
-        iota_f = iota_r.astype(F32)
-
         def gather(i):
-            table = dot_nn(s["t2"][...], s["ol"][:, cols(i)])
-            rows = s["rowi"][rows8(i)]
-            parts = []
-            for r in range(8):
-                column = table[0:64, 128 * r : 128 * r + 128] + table[64:128, 128 * r : 128 * r + 128]
-                parts.append(jnp.sum(jnp.where(iota_f == rows[r : r + 1], column, 0.0), axis=0, keepdims=True))
-            s["frc"][rows8(i)] = s["srcs"][rows8(i)] - BIOT * jnp.concatenate(parts, 0)
-
-        loop(8, gather)
+            index = s["host"][rows8(i)]
+            lanes, rows = index & 127, index >> 7
+            found = jnp.zeros((8, 128), F32)
+            for r in range(64):
+                row = jnp.broadcast_to(s["sti"][r : r + 1], (8, 128))
+                found = jnp.where(rows == r, jnp.take_along_axis(row, lanes, axis=1), found)
+            s["frc"][rows8(i)] = s["srcs"][rows8(i)] - BIOT * found
+
+        loop(8, gather, True)
 
         def residual(p, k):
             return s["frc"][...] + around(p, k) - s["diag"][...] * p[...]
@@ -298,42 +291,37 @@
         wait_halos(s["p2"], 2)
         s["rem"][...] = residual(s["p2"], 2)
 
-        def weighted(i):
-            rem = s["rem"][rows8(i)]
-            highs = []
-            for r in range(8):
-                term = s["wt"][i * 8 + r] * rem[r : r + 1]
-                high = term.astype(BF16).astype(F32)
-                highs.append(jnp.concatenate([high, term - high], 0).astype(BF16))
-            s["wr"][:, cols(i)] = jnp.concatenate(highs, 1)
-
-        loop(8, weighted)
-        coarse = dot_nt(s["wr"][...], s["ob"][...])
-        fixed = (coarse[0:8] + coarse[8:16]) / s["scale"][...]
-        high = fixed.astype(BF16).astype(F32)
-        s["corr"][...] = jnp.concatenate([high, fixed - high], 0).astype(BF16)
-
-        def spread_back(i):
-            back = dot_nn(s["corr"][...], s["ob"][:, cols(i)])
-            back = back[0:8] + back[8:16]
+        coarse = jnp.zeros((16, 64), F32)
+        for i in range(8):
+            rem = s["rem"][8 * i : 8 * i + 8]
             parts = []
             for r in range(8):
-                parts.append(jnp.sum(s["wt"][i * 8 + r] * back[:, 128 * r : 128 * r + 128], axis=0, keepdims=True))
-            updated = s["p2"][rows8(i)] + jnp.concatenate(parts, 0)
-            po[rows8(i)] = updated
-            change = updated - s["pres"][rows8(i)]
+                term = s["wt"][8 * i + r] * rem[r : r + 1]
+                high = term.astype(BF16).astype(F32)
+                parts.append(jnp.concatenate([high, term - high], 0).astype(BF16))
+            coarse = coarse + dot_nt(jnp.concatenate(parts, 1), s["ob"][:, 1024 * i : 1024 * i + 1024])
+        fixed = (coarse[0:8] + coarse[8:16]) / s["scale"][...]
+        table = jnp.concatenate([fixed, fixed], 1)
+        both = jnp.zeros((128, 128), F32)
+        for i in range(8):
+            at = slice(8 * i, 8 * i + 8)
+            blocks_of = s["blk"][at]
+            parts = []
+            for r in range(8):
+                back = jnp.take_along_axis(table, jnp.broadcast_to(blocks_of[r : r + 1], (8, 128)), axis=1)
+                parts.append(jnp.sum(s["wt"][8 * i + r] * back, axis=0, keepdims=True))
+            updated = s["p2"][at] + jnp.concatenate(parts, 0)
+            po[at] = updated
+            change = updated - s["pres"][at]
             high = change.astype(BF16).astype(F32)
             low = change - high
             tops, lows = [], []
             for r in range(8):
-                one = s["oh"][:, pl.ds(pl.multiple_of(i * 1024 + 128 * r, 128), 128)]
+                one = s["oh"][:, 1024 * i + 128 * r : 1024 * i + 128 * r + 128]
                 tops.append(one * jnp.broadcast_to(high[r : r + 1], (64, 128)).astype(BF16))
                 lows.append(one * jnp.broadcast_to(low[r : r + 1], (64, 128)).astype(BF16))
-            s["ar"][0:64, cols(i)] = jnp.concatenate(tops, 1)
-            s["ar"][64:128, cols(i)] = jnp.concatenate(lows, 1)
-
-        loop(8, spread_back)
-        both = dot_nt(s["ar"][...], s["ol"][...])
+            scaled = jnp.concatenate([jnp.concatenate(tops, 1), jnp.concatenate(lows, 1)], 0)
+            both = both + dot_nt(scaled, s["ol"][:, 1024 * i : 1024 * i + 1024])
         s["sm"][...] = both[0:64] + both[64:128]
         start_if(gx >= 0, s["sm"], s["sr"].at[g], SEND_AT["sums"], RECV_AT["sums"] + g, (top, gx, gy))
         do[...] = jnp.zeros((192, 128), F32)
@@ -443,7 +431,7 @@
             mask = jnp.where(sub >= 4, mask * jnp.where(gy == ny - 1, 0.0, 1.0), mask)
         return mask
 
-    def operate(arr, elem_x, elem_j, use):
+    def operate(arr, elem_x, elem_j, use, unroll=True):
         (xa, xb), (ja, jb) = elem_x, elem_j
         ph, plo, vs = s["ph"], s["plo"], s["vs"]
         wide = jb - ja
@@ -457,7 +445,7 @@
                 ph[x, 16 * j : 16 * j + 16] = high
                 plo[x, 16 * j : 16 * j + 16] = low
 
-        loop(xb - xa + 1, stage)
+        loop(xb - xa + 1, stage, unroll)
 
         def elements(k):
             x = xa + k
@@ -472,7 +460,7 @@
                 weight = s["wtile"][x, 8 * j : 8 * j + 8]
                 vs[x, 64 * j : 64 * j + 64] = product[:, 128 * c : 128 * c + 128] * jnp.concatenate([weight] * 8, 0)
 
-        loop(xb - xa, elements)
+        loop(xb - xa, elements, unroll)
 
         spring = SPRING * s["kap"][...]
 
@@ -488,7 +476,7 @@
                 node = arr[x, 8 * j : 8 * j + 8]
                 use(x, j, node, total[0:8] + shift_up(total[8:16]) + spring * node)
 
-        loop(xb - xa - 1, nodes)
+        loop(xb - xa - 1, nodes, unroll)
 
     def mechanics():
         for name in ("disp", "mask", "modl", "stif", "body"):
@@ -629,7 +617,7 @@
         def initial(x, j, node, product):
             ce[x, 8 * j : 8 * j + 8] = s["bt"][x - 2, 8 * (j - 2) : 8 * (j - 2) + 8] - kappa * product
 
-        operate(ue, (1, 6), (1, 10), initial)
+        operate(ue, (1, 6), (1, 10), initial, 1)
         exchange_start(ce_refs, "ce")
         exchange_wait(ce_refs, "ce")
         close_nodes(ce, s["cyl"], s["cyh"])
@@ -657,7 +645,7 @@
             for j in range(13):
                 s["gt"][x, 8 * j : 8 * j + 8] = pair_of_rows(s["gr"], x, 5 + j)
 
-        loop(9, tiles)
+        loop(9, tiles, True)
         part = sub_iota() & 3
         signs = [jnp.where(part == m, -1.0, 1.0).astype(F32) for m in range(3)]
         rx, qe = s["rx"], s["qe"]
@@ -676,7 +664,7 @@
                     rx[x, at] = (ce[x, at] + node) * (y_ok(k) * okay)
                 last = along_x
 
-        loop(8, force)
+        loop(8, force, True)
 
         def first(x, j, node, product):
             qe[x, 8 * j : 8 * j + 8] = product * (y_ok(j) * x_ok(x))
@@ -749,6 +737,14 @@
     pl.when(mech)(mechanics)
 
 
+def hand_over(p_ref, d_ref, p_out, d_out, sems):
+    copies = [pltpu.make_async_copy(p_ref, p_out, sems.at[0]), pltpu.make_async_copy(d_ref, d_out, sems.at[1])]
+    for copy in copies:
+        copy.start()
+    for copy in copies:
+        copy.wait()
+
+
 def local(sizes, *arrays):
     shapes = [(64, 128)] * 5 + [(512, 128), (64, 128), (3, 64, 128), (192, 128), (64, 128), (64, 128), (24, 24)]
     flat = [array.reshape(shape) for array, shape in zip(arrays, shapes)]
@@ -761,12 +757,19 @@
     ]
     pressure, displacement = pl.pallas_call(
         functools.partial(kernel, sizes),
-        out_shape=(jax.ShapeDtypeStruct((64, 128), F32), jax.ShapeDtypeStruct((192, 128), F32)),
+        out_shape=(pltpu.VMEM((64, 128), F32), pltpu.VMEM((192, 128), F32)),
         in_specs=[pl.BlockSpec(memory_space=pl.ANY)] * 12,
         out_specs=(pl.BlockSpec(memory_space=pltpu.VMEM),) * 2,
         scratch_shapes=scratch,
         compiler_params=pltpu.CompilerParams(collective_id=0, has_side_effects=True),
     )(*flat)
+    pressure, displacement = pl.pallas_call(
+        hand_over,
+        out_shape=(jax.ShapeDtypeStruct((64, 128), F32), jax.ShapeDtypeStruct((192, 128), F32)),
+        in_specs=[pl.BlockSpec(memory_space=pltpu.VMEM)] * 2,
+        out_specs=(pl.BlockSpec(memory_space=pl.ANY),) * 2,
+        scratch_shapes=[pltpu.SemaphoreType.DMA((2,))],
+    )(pltpu.with_memory_space_constraint(pressure, pltpu.VMEM), pltpu.with_memory_space_constraint(displacement, pltpu.VMEM))
     return pressure.reshape(arrays[0].shape), displacement.reshape(arrays[7].shape)
 
 

time: 51.6 us -> 43.2 us (0.84)
  Pallas kernels: 47.8 us -> 42.4 us
  local copies, waits for them, and re-layouts: 2.91 us -> 0 us
    pallas_call x1 -> x2, Pallas kernels: 47.8 us -> 42.4 us  [the longest x1 41.8 us: local(): pl.pallas_call(functools.partial(kernel, sizes), out_shape=(pltpu.VMEM((6...]
    unnamed x2 -> x0, local copies, waits for them, and re-layouts: 2.91 us -> none
where the time goes in v2:
time: 43.2 us; the launch traced here: 43.1 us
  Pallas kernels  42.4 us (98%)
  between operations  0.64 us (1%)
    pallas_call x1, Pallas kernels, local(): pl.pallas_call(functools.partial(kernel, sizes), out_shape=(pltpu.VMEM((6...  41.8 us

profile of v2, /device:TPU:24, one launch (start us, length us, event | category | flops | bytes accessed | tf_op | source)
XLA Modules:
  0.0 43.1 jit_solution(11385682336830916551)
XLA Ops:
  0.6 41.8 %shard_map.131 = (f32[64,128]{1,0:T(8,128)S(1)}, f32[192,128]{1,0:T(8,128)S(1)}) custom-call(f32[64,128]{1,0:T(8,128)} %bitcast.16, f32[64,128]{1,0:T(8,128)} %bitcast.17, f32[64,128]{1,0:T(8,128)} %bitcast.18, s32[64,128]{1,0:T(8,128)} %bitcast.19, s32[64,128]{1,0:T(8,128)} %bitcast.20, f32[512,128]{1,0:T(8,128)} %bitcast.13, s32[64,128]{1,0:T(8,128)} %bitcast.21, ...), custom_call_target="tpu_custom_call" | custom-call | tf_op jit(solution)/shard_map/pallas_call | solution.py:758
  42.4 0.7 %shard_map.132 = (f32[64,128]{1,0:T(8,128)}, f32[192,128]{1,0:T(8,128)}) custom-call(f32[64,128]{1,0:T(8,128)S(1)} %get-tuple-element.6.p_ref, f32[192,128]{1,0:T(8,128)S(1)} %get-tuple-element.7.d_ref), custom_call_target="tpu_custom_call" | custom-call | tf_op jit(solution)/shard_map/pallas_call | solution.py:766

commit v3 on v2

--- a/solution.py
+++ b/solution.py
@@ -18,10 +18,10 @@
 RELAX = 0.8
 SPRING = 0.5
 WELL = 4.0
-AROUND = [(dx, dy) for dx in (-1, 0, 1) for dy in (-1, 0, 1) if (dx, dy) != (0, 0)]
-
-SEND = dict(ux=3, strain=3, ue=8, ce=8, mw=8, gr=8, sums=1, counts=1, halo=18, ary=4, arx=16)
-RECV = dict(ux=3, strain=1, ue=8, ce=8, mw=8, gr=8, sums=3, counts=3, halo=18, ary=4, arx=16)
+AROUND = [(-1, -1), (-1, 1), (1, -1), (1, 1), (-1, 0), (1, 0), (0, -1), (0, 1)]
+
+SEND = dict(ux=3, strain=3, ue=8, ce=8, mw=8, gr=8, sums=1, counts=1, halo=18, ar=1)
+RECV = dict(ux=3, strain=1, ue=8, ce=8, mw=8, gr=8, sums=3, counts=3, halo=18, ar=1)
 
 
 def offsets(table):
@@ -57,7 +57,7 @@
     ph=((8, 192, 128), BF16), plo=((8, 192, 128), BF16), vs=((7, 704, 128), F32),
     kl=((64, 192), BF16), kap=((8, 128), F32), bt=((4, 64, 128), F32),
     rr=((192, 128), F32), qr=((192, 128), F32), dots=((8, 128), F32),
-    ar1=((4, 8, 128), F32), ar2=((16, 1, 128), F32), row=((1, 128), F32),
+    ar=((64, 1, 128), F32), row=((1, 128), F32),
 )
 
 
@@ -496,13 +496,42 @@
         pl.semaphore_wait(pltpu.get_barrier_semaphore(), greet_count)
 
         near = [
+            (-1, -1, s["ucs"], s["uc"]),
             (-1, 0, disp.at[:, 0:16], s["ux"]),
             (0, -1, s["uys"], s["uy"]),
-            (-1, -1, s["ucs"], s["uc"]),
         ]
         for k, (dx, dy, src, dst) in enumerate(near):
             start_if(inside(dx, dy), src, dst, SEND_AT["ux"] + k, RECV_AT["ux"] + k, (g, gx + dx, gy + dy))
 
+        rounds, step = [], 1
+        while step < nx:
+            rounds.append((1, step))
+            step *= 2
+        step = 1
+        while step < ny:
+            rounds.append((2, step))
+            step *= 2
+
+        def ends(turn):
+            axis, step = rounds[turn]
+            coord, size = ((gx, nx), (gy, ny))[axis - 1]
+            return coord - step >= 0, coord + step < size
+
+        def call_out(turn):
+            axis, step = rounds[turn]
+            for ok, move in zip(ends(turn), (-step, step)):
+                device = (g, gx + move, gy) if axis == 1 else (g, gx, gy + move)
+
+                @pl.when(ok)
+                def _():
+                    pl.semaphore_signal(known.at[turn], inc=1, device_id=device, device_id_type=MESH)
+
+        def hear(turn):
+            back, ahead = ends(turn)
+            pl.semaphore_wait(known.at[turn], as_int(back) + as_int(ahead))
+
+        call_out(0)
+
         @pl.when(gx == nx - 1)
         def _():
             s["ux"][...] = jnp.zeros((3, 16, 128), F32)
@@ -513,35 +542,10 @@
             s["uy"][...] = jnp.zeros((16, 128), F32)
             s["uc"][...] = jnp.zeros((8, 128), F32)
 
-        local("mask").wait()
-        for k, (dx, dy, _, dst) in enumerate(near):
-            wait_recv_if(inside(-dx, -dy), dst, RECV_AT["ux"] + k)
-
-        row15 = sub_iota((16, 128)) == 15
-        before = None
-        for x in range(5):
-            sums, diffs = [], []
-            for m in range(3):
-                plane = disp[m, 16 * x : 16 * x + 16] if x < 4 else s["ux"][m]
-                beyond = s["uy"][4 * m + x : 4 * m + x + 1] if x < 4 else s["uc"][m : m + 1]
-                up = jnp.where(row15, jnp.broadcast_to(beyond, (16, 128)), pltpu.roll(plane, 15, 0))
-                sums.append(up + plane)
-                diffs.append(up - plane)
-            now = (sums[0], diffs[1], sums[2])
-            if before is not None:
-                plain = (now[0] - before[0]) + (now[1] + before[1])
-                third = now[2] + before[2]
-                value = (plain - third) + shift_down(plain + third)
-                at = 16 * (x - 1)
-                s["stro"][at : at + 16] = 0.25 * s["mask"][at : at + 16].astype(F32) * value
-            before = now
-        for gg in range(top):
-            start_if(gx >= 0, s["stro"], s["sti"], SEND_AT["strain"] + gg, RECV_AT["strain"], (gg, gx, gy))
-
         ue, ce = s["ue"], s["ce"]
         local("modl").wait()
+        local("mask").wait()
         local("body").wait()
-        local("stif").wait()
         zero = jnp.zeros((64, 128), F32)
         for x in range(4):
             ue[x + 2, 16:80] = zero
@@ -565,6 +569,31 @@
         zero_raw(s["mw"])
         zero_raw(s["gr"])
 
+        for k, (dx, dy, _, dst) in enumerate(near):
+            wait_recv_if(inside(-dx, -dy), dst, RECV_AT["ux"] + k)
+
+        row15 = sub_iota((16, 128)) == 15
+        before = None
+        for x in range(5):
+            sums, diffs = [], []
+            for m in range(3):
+                plane = disp[m, 16 * x : 16 * x + 16] if x < 4 else s["ux"][m]
+                beyond = s["uy"][4 * m + x : 4 * m + x + 1] if x < 4 else s["uc"][m : m + 1]
+                up = jnp.where(row15, jnp.broadcast_to(beyond, (16, 128)), pltpu.roll(plane, 15, 0))
+                sums.append(up + plane)
+                diffs.append(up - plane)
+            now = (sums[0], diffs[1], sums[2])
+            if before is not None:
+                plain = (now[0] - before[0]) + (now[1] + before[1])
+                third = now[2] + before[2]
+                value = (plain - third) + shift_down(plain + third)
+                at = 16 * (x - 1)
+                s["stro"][at : at + 16] = 0.25 * s["mask"][at : at + 16].astype(F32) * value
+            before = now
+        for gg in range(top):
+            start_if(gx >= 0, s["stro"], s["sti"], SEND_AT["strain"] + gg, RECV_AT["strain"], (gg, gx, gy))
+
+        local("stif").wait()
         stiff = s["stif"][...]
         largest = jnp.max(jnp.max(jnp.abs(stiff), axis=1, keepdims=True), axis=0, keepdims=True)
         s["kap"][...] = jnp.broadcast_to(1.0 / largest, (8, 128))
@@ -580,21 +609,8 @@
             wide.append(jnp.where(r_half == c_half, dot_nt(rows, pick), 0.0).astype(BF16))
         s["kl"][...] = jnp.concatenate([wide[0], wide[0], wide[1]], 1)
 
-        step, turn = 1, 0
-        for size, coord, axis in ((nx, gx, 1), (ny, gy, 2)):
-            step = 1
-            while step < size:
-                back, ahead = coord - step >= 0, coord + step < size
-                for ok, move in ((back, -step), (ahead, step)):
-                    device = (g, gx + move, gy) if axis == 1 else (g, gx, gy + move)
-
-                    @pl.when(ok)
-                    def _():
-                        pl.semaphore_signal(known.at[turn], inc=1, device_id=device, device_id_type=MESH)
-
-                pl.semaphore_wait(known.at[turn], as_int(back) + as_int(ahead))
-                step, turn = step * 2, turn + 1
-
+        hear(0)
+        call_out(1)
         exchange_wait(mw_refs, "mw")
         half = sub_iota() < 4
 
@@ -617,8 +633,12 @@
         def initial(x, j, node, product):
             ce[x, 8 * j : 8 * j + 8] = s["bt"][x - 2, 8 * (j - 2) : 8 * (j - 2) + 8] - kappa * product
 
-        operate(ue, (1, 6), (1, 10), initial, 1)
+        operate(ue, (1, 6), (1, 10), initial)
         exchange_start(ce_refs, "ce")
+        for turn in range(1, len(rounds)):
+            hear(turn)
+            if turn + 1 < len(rounds):
+                call_out(turn + 1)
         exchange_wait(ce_refs, "ce")
         close_nodes(ce, s["cyl"], s["cyh"])
 
@@ -680,9 +700,13 @@
             acc[0:4] += jnp.concatenate(rows, 0)
 
         operate(qe, (1, 6), (1, 10), second)
-        ar1, ar2 = s["ar1"], s["ar2"]
-        for d in range(1, ny):
-            start_if(gx >= 0, acc, ar1.at[d], SEND_AT["ary"] + d, RECV_AT["ary"] + d, (g, gx, lax.rem(gy + d, ny)))
+        total = jnp.broadcast_to(jnp.sum(acc[...], axis=1, keepdims=True), (8, 128))
+        s["row"][...] = jnp.sum(jnp.where(lane_iota() == sub_iota(), total, 0.0), axis=0, keepdims=True)
+        others = [(dx, dy) for dx in range(nx) for dy in range(ny) if (dx, dy) != (0, 0)]
+        others.sort(key=lambda d: -(min(d[0], nx - d[0]) + 2 * min(d[1], ny - d[1])))
+        for dx, dy in others:
+            device = (g, lax.rem(gx + dx, nx), lax.rem(gy + dy, ny))
+            start_if(gx >= 0, s["row"], s["ar"].at[dx * ny + dy], SEND_AT["ar"], RECV_AT["ar"], device)
 
         def to_rows(arr, out):
             for x in range(4):
@@ -692,19 +716,9 @@
                         out[at : at + 8] = arr[x + 2, pl.ds(16 + 4 * h + m, 8, stride=8), :]
 
         to_rows(rx, s["rr"])
-        total = acc[...]
-        for d in range(1, ny):
-            wait_recv_if(gx >= 0, ar1.at[d], RECV_AT["ary"] + d)
-            total = total + ar1[d]
-        total = jnp.broadcast_to(jnp.sum(total, axis=1, keepdims=True), (8, 128))
-        s["row"][...] = jnp.sum(jnp.where(lane_iota() == sub_iota(), total, 0.0), axis=0, keepdims=True)
-        for d in range(1, nx):
-            start_if(gx >= 0, s["row"], ar2.at[d], SEND_AT["arx"] + d, RECV_AT["arx"] + d, (g, lax.rem(gx + d, nx), gy))
         to_rows(qe, s["qr"])
-        total = s["row"][...]
-        for d in range(1, nx):
-            wait_recv_if(gx >= 0, ar2.at[d], RECV_AT["arx"] + d)
-            total = total + ar2[d]
+        wait_recv_if(gx >= 0, s["ar"].at[1 : nx * ny], RECV_AT["ar"])
+        total = s["row"][...] + jnp.sum(s["ar"][1 : nx * ny], axis=0)
         lane = lane_iota((1, 128))
         aa, bb, cc, ee = [
             jnp.broadcast_to(jnp.sum(jnp.where(lane == k, total, 0.0), axis=1, keepdims=True), (8, 128)) for k in range(4)
@@ -728,10 +742,7 @@
             wait_send_if(gx >= 0, s["stro"], SEND_AT["strain"] + gg)
         for refs_of, name in ((ue_refs, "ue"), (mw_refs, "mw"), (ce_refs, "ce"), (gr_refs, "gr")):
             exchange_done(refs_of, name)
-        for d in range(1, ny):
-            wait_send_if(gx >= 0, acc, SEND_AT["ary"] + d)
-        for d in range(1, nx):
-            wait_send_if(gx >= 0, s["row"], SEND_AT["arx"] + d)
+        wait_send_if(gx >= 0, s["ar"].at[1 : nx * ny], SEND_AT["ar"])
 
     pl.when(jnp.logical_not(mech))(flow)
     pl.when(mech)(mechanics)

time: 43.2 us -> 39.6 us (0.917)
  Pallas kernels: 42.4 us -> 38.9 us
    pallas_call x1, Pallas kernels: 41.8 us -> 38.2 us  [local(): pl.pallas_call(functools.partial(kernel, sizes), out_shape=(pltpu.VMEM((6...]
where the time goes in v3:
time: 39.6 us; the launch traced here: 39.5 us
  Pallas kernels  38.9 us (98%)
  between operations  0.64 us (2%)
    pallas_call x1, Pallas kernels, local(): pl.pallas_call(functools.partial(kernel, sizes), out_shape=(pltpu.VMEM((6...  38.2 us

profile of v3, /device:TPU:24, one launch (start us, length us, event | category | flops | bytes accessed | tf_op | source)
XLA Modules:
  0.0 39.5 jit_solution(3474373306996849999)
XLA Ops:
  0.6 38.2 %shard_map.131 = (f32[64,128]{1,0:T(8,128)S(1)}, f32[192,128]{1,0:T(8,128)S(1)}) custom-call(f32[64,128]{1,0:T(8,128)} %bitcast.16, f32[64,128]{1,0:T(8,128)} %bitcast.17, f32[64,128]{1,0:T(8,128)} %bitcast.18, s32[64,128]{1,0:T(8,128)} %bitcast.19, s32[64,128]{1,0:T(8,128)} %bitcast.20, f32[512,128]{1,0:T(8,128)} %bitcast.13, s32[64,128]{1,0:T(8,128)} %bitcast.21, ...), custom_call_target="tpu_custom_call" | custom-call | tf_op jit(solution)/shard_map/pallas_call | solution.py:769
  38.8 0.7 %shard_map.132 = (f32[64,128]{1,0:T(8,128)}, f32[192,128]{1,0:T(8,128)}) custom-call(f32[64,128]{1,0:T(8,128)S(1)} %get-tuple-element.6.p_ref, f32[192,128]{1,0:T(8,128)S(1)} %get-tuple-element.7.d_ref), custom_call_target="tpu_custom_call" | custom-call | tf_op jit(solution)/shard_map/pallas_call | solution.py:777

commit v4 on v3

--- a/solution.py
+++ b/solution.py
@@ -20,8 +20,8 @@
 WELL = 4.0
 AROUND = [(-1, -1), (-1, 1), (1, -1), (1, 1), (-1, 0), (1, 0), (0, -1), (0, 1)]
 
-SEND = dict(ux=3, strain=3, ue=8, ce=8, mw=8, gr=8, sums=1, counts=1, halo=18, ar=1)
-RECV = dict(ux=3, strain=1, ue=8, ce=8, mw=8, gr=8, sums=3, counts=3, halo=18, ar=1)
+SEND = dict(ux=3, strain=6, ue=8, ce=8, mw=8, gr=8, sums=1, counts=1, halo=18, ar=1)
+RECV = dict(ux=3, strain=2, ue=8, ce=8, mw=8, gr=8, sums=3, counts=3, halo=18, ar=1)
 
 
 def offsets(table):
@@ -55,7 +55,7 @@
     sr=((3, 64, 128), F32), cr=((3, 64, 128), F32), fac=((64, 128), F32),
     gt=((9, 104, 128), F32), rx=((8, 96, 128), F32), qe=((8, 96, 128), F32),
     ph=((8, 192, 128), BF16), plo=((8, 192, 128), BF16), vs=((7, 704, 128), F32),
-    kl=((64, 192), BF16), kap=((8, 128), F32), bt=((4, 64, 128), F32),
+    kl=((64, 192), BF16), pf=((8, 192, 128), F32), gys=((2, 8, 128), F32), gyr=((6, 8, 128), F32), kap=((8, 128), F32), bt=((4, 64, 128), F32),
     rr=((192, 128), F32), qr=((192, 128), F32), dots=((8, 128), F32),
     ar=((64, 1, 128), F32), row=((1, 128), F32),
 )
@@ -261,17 +261,17 @@
             s["wr"][:, cols(i)] = jnp.concatenate(highs, 1)
 
         loop(8, blocks)
-        wait_recv_if(gx >= 0, s["sti"], RECV_AT["strain"])
-        def gather(i):
-            index = s["host"][rows8(i)]
-            lanes, rows = index & 127, index >> 7
-            found = jnp.zeros((8, 128), F32)
-            for r in range(64):
-                row = jnp.broadcast_to(s["sti"][r : r + 1], (8, 128))
-                found = jnp.where(rows == r, jnp.take_along_axis(row, lanes, axis=1), found)
-            s["frc"][rows8(i)] = s["srcs"][rows8(i)] - BIOT * found
-
-        loop(8, gather, True)
+        for half in range(2):
+            wait_recv_if(gx >= 0, s["sti"].at[32 * half : 32 * half + 32], RECV_AT["strain"] + half)
+            for i in range(8):
+                at = slice(8 * i, 8 * i + 8)
+                index = s["host"][at]
+                lanes, rows = index & 127, index >> 7
+                found = s["frc"][at] if half else jnp.zeros((8, 128), F32)
+                for r in range(32 * half, 32 * half + 32):
+                    row = jnp.broadcast_to(s["sti"][r : r + 1], (8, 128))
+                    found = jnp.where(rows == r, jnp.take_along_axis(row, lanes, axis=1), found)
+                s["frc"][at] = s["srcs"][at] - BIOT * found if half else found
 
         def residual(p, k):
             return s["frc"][...] + around(p, k) - s["diag"][...] * p[...]
@@ -353,6 +353,12 @@
         ysrc, ydst = {0: (slice(8, 24), slice(8, 24)), 1: (slice(16, 24), slice(0, 8)), -1: (slice(8, 16), slice(24, 32))}[dy]
         return arr.at[xs, ysrc], arr.at[xd, ydst]
 
+    def pressure_refs(dx, dy):
+        if dy:
+            return s["gys"].at[0 if dy < 0 else 1], s["gyr"].at[(3 if dy < 0 else 0) + dx + 1]
+        src, dst = (slice(3, 5), slice(7, 9)) if dx < 0 else (slice(5, 7), slice(1, 3))
+        return s["gr"].at[src, 8:24], s["gr"].at[dst, 8:24]
+
     def exchange_start(refs_of, name):
         for k, (dx, dy) in enumerate(AROUND):
             src, dst = refs_of(dx, dy)
@@ -431,36 +437,35 @@
             mask = jnp.where(sub >= 4, mask * jnp.where(gy == ny - 1, 0.0, 1.0), mask)
         return mask
 
-    def operate(arr, elem_x, elem_j, use, unroll=True):
-        (xa, xb), (ja, jb) = elem_x, elem_j
-        ph, plo, vs = s["ph"], s["plo"], s["vs"]
-        wide = jb - ja
-
-        def stage(k):
-            x = xa + k
-            for j in range(ja, jb + 1):
+    def stage_nodes(arr, elem_x, elem_j, keep):
+        for x in range(elem_x[0], elem_x[1] + 1):
+            for j in range(elem_j[0], elem_j[1] + 1):
                 value = arr[x, 8 * j : 8 * j + 8]
                 pair = jnp.concatenate([value, shift_down(value)], 0)
+                if keep:
+                    s["pf"][x, 16 * j : 16 * j + 16] = pair
                 high, low = split(pair)
-                ph[x, 16 * j : 16 * j + 16] = high
-                plo[x, 16 * j : 16 * j + 16] = low
-
-        loop(xb - xa + 1, stage, unroll)
-
-        def elements(k):
-            x = xa + k
-            columns = []
-            for j in range(ja, jb):
-                at = slice(16 * j, 16 * j + 32)
-                first, second = ph[x, at], ph[x + 1, at]
-                columns.append(jnp.concatenate([first, second, plo[x, at], plo[x + 1, at], first, second], 0))
-            product = dot_nn(s["kl"][...], jnp.concatenate(columns, 1))
-            for c in range(wide):
+                s["ph"][x, 16 * j : 16 * j + 16] = high
+                s["plo"][x, 16 * j : 16 * j + 16] = low
+
+    def element_product(x, elem_j):
+        columns = []
+        for j in range(*elem_j):
+            at = slice(16 * j, 16 * j + 32)
+            first, second = s["ph"][x, at], s["ph"][x + 1, at]
+            columns.append(jnp.concatenate([first, second, s["plo"][x, at], s["plo"][x + 1, at], first, second], 0))
+        return dot_nn(s["kl"][...], jnp.concatenate(columns, 1))
+
+    def operate(arr, elem_x, elem_j, use):
+        (xa, xb), (ja, jb) = elem_x, elem_j
+        vs = s["vs"]
+        stage_nodes(arr, elem_x, elem_j, False)
+        for x in range(xa, xb):
+            product = element_product(x, elem_j)
+            for c in range(jb - ja):
                 j = ja + c
                 weight = s["wtile"][x, 8 * j : 8 * j + 8]
                 vs[x, 64 * j : 64 * j + 64] = product[:, 128 * c : 128 * c + 128] * jnp.concatenate([weight] * 8, 0)
-
-        loop(xb - xa, elements, unroll)
 
         spring = SPRING * s["kap"][...]
 
@@ -476,11 +481,12 @@
                 node = arr[x, 8 * j : 8 * j + 8]
                 use(x, j, node, total[0:8] + shift_up(total[8:16]) + spring * node)
 
-        loop(xb - xa - 1, nodes, unroll)
+        loop(xb - xa - 1, nodes, True)
 
     def mechanics():
         for name in ("disp", "mask", "modl", "stif", "body"):
             local(name).start()
+        s["gyr"][...] = jnp.zeros((6, 8, 128), F32)
         greet_count = I32(top)
         for gg in range(top):
             greet(gx >= 0, (gg, gx, gy))
@@ -561,7 +567,7 @@
         ue_refs = functools.partial(node_refs, ue, s["uyl"], s["uyh"])
         ce_refs = functools.partial(node_refs, ce, s["cyl"], s["cyh"])
         mw_refs = functools.partial(raw_refs, s["mw"])
-        gr_refs = functools.partial(raw_refs, s["gr"])
+        gr_refs = pressure_refs
         exchange_start(ue_refs, "ue")
         exchange_start(mw_refs, "mw")
         zero_edges(ue, s["uyl"], s["uyh"])
@@ -590,8 +596,10 @@
                 at = 16 * (x - 1)
                 s["stro"][at : at + 16] = 0.25 * s["mask"][at : at + 16].astype(F32) * value
             before = now
-        for gg in range(top):
-            start_if(gx >= 0, s["stro"], s["sti"], SEND_AT["strain"] + gg, RECV_AT["strain"], (gg, gx, gy))
+        for half in range(2):
+            at = slice(32 * half, 32 * half + 32)
+            for gg in sorted(range(top), key=lambda gg: -min(top - gg, gg + 1)):
+                start_if(gx >= 0, s["stro"].at[at], s["sti"].at[at], SEND_AT["strain"] + 2 * gg + half, RECV_AT["strain"] + half, (gg, gx, gy))
 
         local("stif").wait()
         stiff = s["stif"][...]
@@ -658,48 +666,64 @@
         value = s["fac"][...] * sums
         for x in range(4):
             s["gr"][x + 3, 8:24] = value[16 * x : 16 * x + 16]
+            s["gys"][0, 2 * x : 2 * x + 2] = value[16 * x : 16 * x + 2]
+            s["gys"][1, 2 * x : 2 * x + 2] = value[16 * x + 14 : 16 * x + 16]
         exchange_start(gr_refs, "gr")
         exchange_wait(gr_refs, "gr")
-
-        def tiles(x):
-            for j in range(13):
-                s["gt"][x, 8 * j : 8 * j + 8] = pair_of_rows(s["gr"], x, 5 + j)
-
-        loop(9, tiles, True)
+        for side in range(2):
+            for dx, planes in ((-1, (0, 1)), (0, (0, 1, 2, 3)), (1, (2, 3))):
+                for x in planes:
+                    to = 24 if side else 6
+                    s["gr"][x + 3 - 4 * dx, to : to + 2] = s["gyr"][3 * side + dx + 1, 2 * x : 2 * x + 2]
+
+        def tiles(k):
+            for j in range(1, 13):
+                s["gt"][k + 1, 8 * j : 8 * j + 8] = pair_of_rows(s["gr"], k + 1, 5 + j)
+
+        loop(8, tiles, True)
         part = sub_iota() & 3
         signs = [jnp.where(part == m, -1.0, 1.0).astype(F32) for m in range(3)]
         rx, qe = s["rx"], s["qe"]
 
-        def force(x):
+        def force(k):
+            x = k + 1
             okay = x_ok(x)
             last = None
-            for j in range(13):
+            for j in range(1, 13):
                 at = slice(8 * j, 8 * j + 8)
                 along_x = s["gt"][x, at] + signs[0] * s["gt"][x + 1, at]
                 if last is not None:
                     both = last + signs[1] * along_x
                     node = shift_up(both) + signs[2] * both
-                    k = j - 1
-                    at = slice(8 * k, 8 * k + 8)
-                    rx[x, at] = (ce[x, at] + node) * (y_ok(k) * okay)
+                    at = slice(8 * j - 8, 8 * j)
+                    rx[x, at] = (ce[x, at] + node) * (y_ok(j - 1) * okay)
                 last = along_x
 
-        loop(8, force, True)
+        loop(7, force, True)
 
         def first(x, j, node, product):
             qe[x, 8 * j : 8 * j + 8] = product * (y_ok(j) * x_ok(x))
 
-        operate(rx, (0, 7), (0, 11), first)
+        operate(rx, (1, 7), (1, 11), first)
+        sums = [jnp.zeros((8, 128), F32) for _ in range(4)]
+        for x in range(2, 6):
+            for j in range(2, 10):
+                r, q = rx[x, 8 * j : 8 * j + 8], qe[x, 8 * j : 8 * j + 8]
+                for k, term in enumerate((r * r, r * q, q * q)):
+                    sums[k] = sums[k] + term
+        stage_nodes(qe, (2, 6), (2, 10), True)
+        for x in range(2, 6):
+            product = element_product(x, (2, 10))
+            for c in range(8):
+                j = 2 + c
+                at = slice(16 * j, 16 * j + 32)
+                work = product[:, 128 * c : 128 * c + 128] * jnp.concatenate([s["pf"][x, at], s["pf"][x + 1, at]], 0)
+                total = work[0:8]
+                for k in range(1, 8):
+                    total = total + work[8 * k : 8 * k + 8]
+                sums[3] = sums[3] + total * s["wtile"][x, 8 * j : 8 * j + 8]
         acc = s["dots"]
-        acc[...] = jnp.zeros((8, 128), F32)
-
-        def second(x, j, node, product):
-            r = rx[x, 8 * j : 8 * j + 8]
-            terms = [r * r, r * node, node * node, node * product]
-            rows = [jnp.sum(term, axis=0, keepdims=True) for term in terms]
-            acc[0:4] += jnp.concatenate(rows, 0)
-
-        operate(qe, (1, 6), (1, 10), second)
+        acc[...] = jnp.concatenate([jnp.sum(term, axis=0, keepdims=True) for term in sums] + [jnp.zeros((4, 128), F32)], 0)
         total = jnp.broadcast_to(jnp.sum(acc[...], axis=1, keepdims=True), (8, 128))
         s["row"][...] = jnp.sum(jnp.where(lane_iota() == sub_iota(), total, 0.0), axis=0, keepdims=True)
         others = [(dx, dy) for dx in range(nx) for dy in range(ny) if (dx, dy) != (0, 0)]
@@ -723,12 +747,13 @@
         aa, bb, cc, ee = [
             jnp.broadcast_to(jnp.sum(jnp.where(lane == k, total, 0.0), axis=1, keepdims=True), (8, 128)) for k in range(4)
         ]
+        inverse = s["kap"][...]
+        ee = ee + SPRING * inverse * cc
         step0 = aa / bb
         new = step0 * step0 * cc - aa
         along = bb - 2.0 * step0 * cc + step0 * step0 * ee
         ratio = new / aa
         step1 = new / (along - ratio * new / step0)
-        inverse = s["kap"][...]
         alpha = (step0 + step1 * (1.0 + ratio)) * inverse
         gamma = step1 * step0 * inverse
         for k in range(24):
@@ -738,8 +763,8 @@
 
         for k, (dx, dy, src, _) in enumerate(near):
             wait_send_if(inside(dx, dy), src, SEND_AT["ux"] + k)
-        for gg in range(top):
-            wait_send_if(gx >= 0, s["stro"], SEND_AT["strain"] + gg)
+        for k in range(2 * top):
+            wait_send_if(gx >= 0, s["stro"].at[0:32], SEND_AT["strain"] + k)
         for refs_of, name in ((ue_refs, "ue"), (mw_refs, "mw"), (ce_refs, "ce"), (gr_refs, "gr")):
             exchange_done(refs_of, name)
         wait_send_if(gx >= 0, s["ar"].at[1 : nx * ny], SEND_AT["ar"])

time: 39.6 us -> 38.8 us (0.980)
  Pallas kernels: 38.9 us -> 38 us
    pallas_call x1, Pallas kernels: 38.2 us -> 37.3 us  [local(): pl.pallas_call(functools.partial(kernel, sizes), out_shape=(pltpu.VMEM((6...]
where the time goes in v4:
time: 38.8 us; the launch traced here: 38.7 us
  Pallas kernels  38 us (98%)
  between operations  0.64 us (2%)
    pallas_call x1, Pallas kernels, local(): pl.pallas_call(functools.partial(kernel, sizes), out_shape=(pltpu.VMEM((6...  37.3 us

profile of v4, /device:TPU:24, one launch (start us, length us, event | category | flops | bytes accessed | tf_op | source)
XLA Modules:
  0.0 38.7 jit_solution(4257463356339203357)
XLA Ops:
  0.6 37.3 %shard_map.131 = (f32[64,128]{1,0:T(8,128)S(1)}, f32[192,128]{1,0:T(8,128)S(1)}) custom-call(f32[64,128]{1,0:T(8,128)} %bitcast.16, f32[64,128]{1,0:T(8,128)} %bitcast.17, f32[64,128]{1,0:T(8,128)} %bitcast.18, s32[64,128]{1,0:T(8,128)} %bitcast.19, s32[64,128]{1,0:T(8,128)} %bitcast.20, f32[512,128]{1,0:T(8,128)} %bitcast.13, s32[64,128]{1,0:T(8,128)} %bitcast.21, ...), custom_call_target="tpu_custom_call" | custom-call | tf_op jit(solution)/shard_map/pallas_call | solution.py:794
  38.0 0.7 %shard_map.132 = (f32[64,128]{1,0:T(8,128)}, f32[192,128]{1,0:T(8,128)}) custom-call(f32[64,128]{1,0:T(8,128)S(1)} %get-tuple-element.6.p_ref, f32[192,128]{1,0:T(8,128)S(1)} %get-tuple-element.7.d_ref), custom_call_target="tpu_custom_call" | custom-call | tf_op jit(solution)/shard_map/pallas_call | solution.py:802

commit v5 on v4

--- a/solution.py
+++ b/solution.py
@@ -61,6 +61,9 @@
 )
 
 
+STRAIN_PARTS = (slice(0, 48), slice(48, 64))
+
+
 def split(value):
     high = value.astype(BF16)
     return high, (value - high.astype(F32)).astype(BF16)
@@ -261,14 +264,14 @@
             s["wr"][:, cols(i)] = jnp.concatenate(highs, 1)
 
         loop(8, blocks)
-        for half in range(2):
-            wait_recv_if(gx >= 0, s["sti"].at[32 * half : 32 * half + 32], RECV_AT["strain"] + half)
+        for half, part in enumerate(STRAIN_PARTS):
+            wait_recv_if(gx >= 0, s["sti"].at[part], RECV_AT["strain"] + half)
             for i in range(8):
                 at = slice(8 * i, 8 * i + 8)
                 index = s["host"][at]
                 lanes, rows = index & 127, index >> 7
                 found = s["frc"][at] if half else jnp.zeros((8, 128), F32)
-                for r in range(32 * half, 32 * half + 32):
+                for r in range(part.start, part.stop):
                     row = jnp.broadcast_to(s["sti"][r : r + 1], (8, 128))
                     found = jnp.where(rows == r, jnp.take_along_axis(row, lanes, axis=1), found)
                 s["frc"][at] = s["srcs"][at] - BIOT * found if half else found
@@ -575,12 +578,23 @@
         zero_raw(s["mw"])
         zero_raw(s["gr"])
 
-        for k, (dx, dy, _, dst) in enumerate(near):
-            wait_recv_if(inside(-dx, -dy), dst, RECV_AT["ux"] + k)
-
+        def await_near(*which):
+            for k in which:
+                dx, dy, _, dst = near[k]
+                wait_recv_if(inside(-dx, -dy), dst, RECV_AT["ux"] + k)
+
+        def send_strain(half):
+            part = STRAIN_PARTS[half]
+            for gg in sorted(range(top), key=lambda gg: -min(top - gg, gg + 1)):
+                start_if(gx >= 0, s["stro"].at[part], s["sti"].at[part], SEND_AT["strain"] + 2 * gg + half, RECV_AT["strain"] + half, (gg, gx, gy))
+
+        await_near(2)
         row15 = sub_iota((16, 128)) == 15
         before = None
         for x in range(5):
+            if x == 4:
+                send_strain(0)
+                await_near(0, 1)
             sums, diffs = [], []
             for m in range(3):
                 plane = disp[m, 16 * x : 16 * x + 16] if x < 4 else s["ux"][m]
@@ -596,11 +610,7 @@
                 at = 16 * (x - 1)
                 s["stro"][at : at + 16] = 0.25 * s["mask"][at : at + 16].astype(F32) * value
             before = now
-        for half in range(2):
-            at = slice(32 * half, 32 * half + 32)
-            for gg in sorted(range(top), key=lambda gg: -min(top - gg, gg + 1)):
-                start_if(gx >= 0, s["stro"].at[at], s["sti"].at[at], SEND_AT["strain"] + 2 * gg + half, RECV_AT["strain"] + half, (gg, gx, gy))
-
+        send_strain(1)
         local("stif").wait()
         stiff = s["stif"][...]
         largest = jnp.max(jnp.max(jnp.abs(stiff), axis=1, keepdims=True), axis=0, keepdims=True)
@@ -763,8 +773,9 @@
 
         for k, (dx, dy, src, _) in enumerate(near):
             wait_send_if(inside(dx, dy), src, SEND_AT["ux"] + k)
-        for k in range(2 * top):
-            wait_send_if(gx >= 0, s["stro"].at[0:32], SEND_AT["strain"] + k)
+        for half, part in enumerate(STRAIN_PARTS):
+            for gg in range(top):
+                wait_send_if(gx >= 0, s["stro"].at[part], SEND_AT["strain"] + 2 * gg + half)
         for refs_of, name in ((ue_refs, "ue"), (mw_refs, "mw"), (ce_refs, "ce"), (gr_refs, "gr")):
             exchange_done(refs_of, name)
         wait_send_if(gx >= 0, s["ar"].at[1 : nx * ny], SEND_AT["ar"])

time: 38.8 us -> 38.5 us (level)
  no operation moved by 1% of the time
where the time goes in v5:
time: 38.5 us; the launch traced here: 38.4 us
  Pallas kernels  37.8 us (98%)
  between operations  0.64 us (2%)
    pallas_call x1, Pallas kernels, local(): pl.pallas_call(functools.partial(kernel, sizes), out_shape=(pltpu.VMEM((6...  37.1 us

profile of v5, /device:TPU:24, one launch (start us, length us, event | category | flops | bytes accessed | tf_op | source)
XLA Modules:
  0.0 38.4 jit_solution(15914558179264323869)
XLA Ops:
  0.6 37.1 %shard_map.131 = (f32[64,128]{1,0:T(8,128)S(1)}, f32[192,128]{1,0:T(8,128)S(1)}) custom-call(f32[64,128]{1,0:T(8,128)} %bitcast.16, f32[64,128]{1,0:T(8,128)} %bitcast.17, f32[64,128]{1,0:T(8,128)} %bitcast.18, s32[64,128]{1,0:T(8,128)} %bitcast.19, s32[64,128]{1,0:T(8,128)} %bitcast.20, f32[512,128]{1,0:T(8,128)} %bitcast.13, s32[64,128]{1,0:T(8,128)} %bitcast.21, ...), custom_call_target="tpu_custom_call" | custom-call | tf_op jit(solution)/shard_map/pallas_call | solution.py:805
  37.8 0.7 %shard_map.132 = (f32[64,128]{1,0:T(8,128)}, f32[192,128]{1,0:T(8,128)}) custom-call(f32[64,128]{1,0:T(8,128)S(1)} %get-tuple-element.6.p_ref, f32[192,128]{1,0:T(8,128)S(1)} %get-tuple-element.7.d_ref), custom_call_target="tpu_custom_call" | custom-call | tf_op jit(solution)/shard_map/pallas_call | solution.py:813
